TPU v7x, 256 devices: a whole 4x4x8 slice. The times are simulated.
256 devices in a mesh: grid: 32 (over y, x, core), rows: 8 (over z).
Axes of the slice: x: 4, y: 4, z: 8, core: 2. Of those that a mesh axis runs over, the one named last changes fastest.
Arguments:
- density: bfloat16 [32, 128, 4096], P(None, 'rows', 'grid'), as said below
- basis_values: bfloat16 [64, 16, 128, 512], P('grid', None, 'rows'), may hold values from -0.59765625 to 0.59765625
- grid_points: float32 [64, 3, 512], P('grid'), may hold values from -4 to 4
- grid_weights: float32 [64, 512], P('grid'), may hold values from 0.05 to 1
- screened_blocks: int32 [64, 16], P('grid'), may hold values from 0 to 31, as said below
Outputs:
- exchange: float32 [32, 128, 4096], P(None, 'rows', 'grid')
Inputs may be any that keep to these rules, and one draw needn't show every extreme that they name: density is symmetric: density[a, i, b * 128 + j] equals density[b, j, a * 128 + i]. `screened_blocks`: each row holds 16 distinct block numbers.
All inputs are finite; a program needn't handle non-finite values.
Results may differ from a plain program's by a relative error of at most 0.00055.
The roundings to bfloat16 on the way count: a program that leaves them out, or rounds other values in their place, can miss the bound.
Values may be sent and summed in bfloat16 or wider, within the bound.
A program may use at most 64 MiB of HBM per device.

v0:
```python
import jax
import jax.numpy as jnp
from jax import lax
from jax.sharding import PartitionSpec as P


def copy_for_each(shard, axis):
    copies = jnp.broadcast_to(shard, (lax.axis_size(axis), *shard.shape))
    return lax.all_to_all(copies, axis, split_axis=0, concat_axis=0, tiled=True)


def joined_along(blocks, dim):
    shape = list(blocks.shape[1:])
    shape[dim] *= blocks.shape[0]
    return jnp.moveaxis(blocks, 0, dim).reshape(shape)


def gather_directly(shard, axis, dim):
    blocks = copy_for_each(shard, axis)
    return joined_along(blocks, dim)


def body(density, basis_values, grid_points, grid_weights, screened_blocks):
    nblocks = density.shape[0]
    rows_mine = density.shape[1]
    block_size = rows_mine * lax.axis_size("rows")
    nbasis = nblocks * block_size
    nsig = basis_values.shape[1]
    npoints = basis_values.shape[3]
    stripe = lax.all_gather(density, "grid", axis=2, tiled=True)
    totals = jnp.zeros((nblocks, rows_mine, nblocks, block_size), jnp.float32)
    for batch_index in range(basis_values.shape[0]):
        blocks = screened_blocks[batch_index]
        row_pick = jnp.take(stripe, blocks, axis=0).reshape(nsig * rows_mine, nblocks, block_size)
        chosen = jnp.take(row_pick, blocks, axis=1)
        local_values = basis_values[batch_index]
        x_mine = local_values.reshape(nsig * rows_mine, npoints)
        fsum = jnp.einsum(
            "mtk,tkp->mp",
            chosen,
            gather_directly(local_values, "rows", 1),
            preferred_element_type=jnp.float32,
        )
        fmat = fsum.astype(jnp.bfloat16)
        intersection_part = lax.dot_general(
            x_mine, fmat, (((0,), (0,)), ((), ())), preferred_element_type=jnp.float32
        )
        intersection = lax.psum(intersection_part, "rows")
        places = grid_points[batch_index]
        weights = grid_weights[batch_index]
        diffs = places[:, :, None] - places[:, None, :]
        kern = 1.0 / jnp.sqrt(jnp.sum(diffs * diffs, axis=0) + 0.5)
        mixed = (weights[:, None] * kern * intersection).astype(jnp.bfloat16)
        potential = (
            jnp.dot(x_mine, mixed, preferred_element_type=jnp.float32) * weights[None, :]
        ).astype(jnp.bfloat16)
        potential = potential.reshape(nsig, rows_mine, npoints)
        block_k = jnp.einsum(
            "mp,tkp->mtk",
            x_mine,
            lax.all_gather(potential, "rows", axis=1, tiled=True),
            preferred_element_type=jnp.float32,
        )
        block_k = block_k.reshape(nsig, rows_mine, nsig, block_size)
        totals = totals.at[blocks[:, None], :, blocks[None, :], :].add(
            block_k.transpose(0, 2, 1, 3)
        )
    return lax.psum_scatter(
        totals.reshape(nblocks, rows_mine, nbasis), "grid", scatter_dimension=2, tiled=True
    )


def solution(mesh):
    placed = (
        P(None, "rows", "grid"),
        P("grid", None, "rows", None),
        P("grid", None, None),
        P("grid", None),
        P("grid", None),
    )
    return jax.shard_map(
        body, mesh=mesh, in_specs=placed, out_specs=P(None, "rows", "grid"), check_vma=False
    )
```

profile of v0, /device:TPU:96, one launch (start us, length us, event | category | flops | bytes accessed | tf_op | source)
XLA Modules:
  0.0 493.9 jit_solution(1196830963108560420)
XLA Ops:
  8.6 55.2 %all_to_all.10 = bf16[8,16,16,512]{3,2,1,0:T(8,128)(2,1)} all-to-all(bf16[8,16,16,512]{3,2,1,0:T(8,128)(2,1)S(1)} %broadcast_in_dim.59), channel_id=1, replica_groups=mesh['grid'=32,'rows'=8] {'rows'}, dimensions={0} | all-to-all | bytes 4194304 | tf_op jit(solution)/shard_map/all_to_all | solution.py:9
  65.4 7.3 %all-to-all-start = ((bf16[8,16,16,512]{3,2,1,0:T(8,128)(2,1)}), bf16[8,16,16,512]{3,2,1,0:T(8,128)(2,1)S(1)}, u32[]{:S(2)}, u32[]{:S(2)}) async-start(bf16[8,16,16,512]{3,2,1,0:T(8,128)(2,1)} %broadcast_in_dim.55), calls=%async_computation | async-start | bytes 4194304 | tf_op jit(solution)/shard_map/all_to_all | solution.py:9
  72.7 3.2 copy.34
  75.9 41.9 %all-to-all-done = bf16[8,16,16,512]{3,2,1,0:T(8,128)(2,1)S(1)} async-done(((bf16[8,16,16,512]{3,2,1,0:T(8,128)(2,1)}), bf16[8,16,16,512]{3,2,1,0:T(8,128)(2,1)S(1)}, u32[]{:S(2)}, u32[]{:S(2)}) %all-to-all-start) | async-done | bytes 2097184 | tf_op jit(solution)/shard_map/all_to_all | solution.py:9
  119.3 2.9 gather_fusion.2
  125.5 2.9 gather_fusion
  131.6 4.1 convolution_bitcast_fusion.2
  135.7 3.3 convolution_bitcast_fusion.3
  140.4 80.8 %all-reduce.3.cloned.1.call-done = (f32[512,512]{0,1:T(8,128)}, f32[512,512]{0,1:T(8,128)}) async-done(((f32[512,512]{0,1:T(8,128)}, f32[512,512]{0,1:T(8,128)}), (f32[512,512]{0,1:T(8,128)}, f32[512,512]{0,1:T(8,128)})) %all-reduce.3.cloned.1.call-update) | async-done | bytes 2097168 | tf_op jit(solution)/shard_map/psum | solution.py:48
  221.2 2.3 fusion
  224.3 2.3 fusion.1
  227.2 36.7 %all-gather.6.cloned.1.call-done = bf16[16,128,512]{2,1,0:T(8,128)(2,1)} async-done(((bf16[16,16,512]{2,1,0:T(8,128)(2,1)}), bf16[16,128,512]{2,1,0:T(8,128)(2,1)}) %all-gather.6.cloned.1.call-update) | async-done | bytes 2097168 | tf_op jit(solution)/shard_map/all_gather | solution.py:61
  263.9 2.3 convolution_bitcast_fusion.1
  266.2 2.0 copy.30
  268.2 2.3 copy.31
  270.5 34.5 %all-gather.8.cloned.1.call-done = bf16[16,128,512]{2,1,0:T(8,128)(2,1)} async-done(((bf16[16,16,512]{2,1,0:T(8,128)(2,1)}), bf16[16,128,512]{2,1,0:T(8,128)(2,1)}) %all-gather.8.cloned.1.call-update) | async-done | bytes 2097168 | tf_op jit(solution)/shard_map/all_gather | solution.py:61
  305.0 3.6 convolution_bitcast_fusion
  308.6 3.1 copy.35
  311.7 3.6 copy.36
  315.3 4.2 broadcast_in_dim.51
  319.5 28.4 %scatter_fusion = f32[32,16,32,128]{3,1,2,0:T(8,128)} fusion(f32[32,16,32,128]{3,1,2,0:T(8,128)} %broadcast_in_dim.51, s32[256]{0:T(256)S(1)} %reshape.140, f32[256,16,128]{2,1,0:T(8,128)S(1)} %bitcast.107), kind=kCustom, calls=%fused_computation.4 | custom fusion | flops 524288 | bytes 6293504 | tf_op jit(solution)/shard_map/scatter-add | solution.py:65
  347.9 31.8 %scatter_fusion.1 = f32[32,16,32,128]{3,1,2,0:T(8,128)} fusion(f32[32,16,32,128]{3,1,2,0:T(8,128)} %scatter_fusion, s32[256]{0:T(256)S(1)} %reshape.146, f32[256,16,128]{2,1,0:T(8,128)} %bitcast.108), kind=kCustom, calls=%fused_computation.5 | custom fusion | flops 524288 | bytes 6293504 | tf_op jit(solution)/shard_map/scatter-add | solution.py:65
  379.7 7.8 %copy_bitcast_fusion = f32[32,16,4096]{2,1,0:T(8,128)} fusion(f32[32,16,32,128]{3,1,2,0:T(8,128)} %scatter_fusion.1), kind=kLoop, calls=%fused_computation.6 | loop fusion | bytes 16777216 | tf_op jit(solution)/shard_map/reshape | solution.py:69
  387.4 99.9 %reduce-scatter.2.cloned.1.call-done = f32[32,16,128]{2,1,0:T(8,128)} async-done(((f32[32,16,4096]{2,1,0:T(8,128)}), f32[32,16,128]{2,1,0:T(8,128)}) %reduce-scatter.2.cloned.1.call-update) | async-done | bytes 262160 | tf_op jit(solution)/shard_map/reduce_scatter | solution.py:68
  (49 shorter events, 14.5 us)
Async XLA Ops:
  6.5 112.8 %all-gather.4.cloned.1.call-start = ((), (), s32[]{:S(2)}) async-start(), calls=%async_computation.3 | async-start | bytes 4325376 | tf_op jit(solution)/shard_map/all_gather | solution.py:30
  65.4 7.3 %copy-start.3 = (s32[2,16]{1,0:T(2,128)S(1)}, s32[2,16]{1,0:T(2,128)}, u32[]{:S(2)}) copy-start(s32[2,16]{1,0:T(2,128)} %param.13) | copy-start | bytes 388
  65.4 52.3 %all-to-all-start = ((bf16[8,16,16,512]{3,2,1,0:T(8,128)(2,1)}), bf16[8,16,16,512]{3,2,1,0:T(8,128)(2,1)S(1)}, u32[]{:S(2)}, u32[]{:S(2)}) async-start(bf16[8,16,16,512]{3,2,1,0:T(8,128)(2,1)} %broadcast_in_dim.55), calls=%async_computation | async-start | bytes 4194304 | tf_op jit(solution)/shard_map/all_to_all | solution.py:9
  72.6 148.6 %all-reduce.3.cloned.1.call-start = ((), (), s32[]{:S(2)}) async-start(), calls=%async_computation.7 | async-start | bytes 4194304 | tf_op jit(solution)/shard_map/psum | solution.py:48
  131.6 4.1 copy-start
  139.0 0.7 copy-start.1
  139.0 1.4 copy-start.2
  139.0 124.9 %all-gather.6.cloned.1.call-start = ((), (), s32[]{:S(2)}) async-start(), calls=%async_computation.4 | async-start | bytes 2359296 | tf_op jit(solution)/shard_map/all_gather | solution.py:61
  223.5 81.4 %all-gather.8.cloned.1.call-start = ((), (), s32[]{:S(2)}) async-start(), calls=%async_computation.5 | async-start | bytes 2359296 | tf_op jit(solution)/shard_map/all_gather | solution.py:61
  226.6 260.7 %reduce-scatter.2.cloned.1.call-start = ((), (), s32[]{:S(2)}) async-start(), calls=%async_computation.6 | async-start | bytes 8650752 | tf_op jit(solution)/shard_map/reduce_scatter | solution.py:68
Sparse Core Ops, SparseCore 0:
  9.8 55.4 all-gather.3
  139.1 82.0 all-reduce.2
  223.7 40.1 all-gather.5
  265.5 39.4 all-gather.7
  387.6 99.7 reduce-scatter.1
where the time goes:
time: 496 us; the launch traced here: 494 us
  waiting for transfers between devices  295 us (59%)
  other arithmetic  61.5 us (12%)
  blocking collectives  55.2 us (11%)
  local copies, waits for them, and re-layouts  43.8 us (9%)
  matrix products  17.9 us (4%)
  between operations  13.4 us (3%)
  starting transfers between devices  7.56 us (2%)
    reduce_scatter x1, waiting for transfers between devices, body(): lax.psum_scatter(totals.reshape(nblocks, rows_mine, nbasis), 'grid', scat...  99.9 us
    psum x1, waiting for transfers between devices, body(): intersection = lax.psum(intersection_part, 'rows')  80.8 us
    all_gather x2, waiting for transfers between devices, body(): lax.all_gather(potential, 'rows', axis=1, tiled=True)  71.2 us
    scatter-add x2, other arithmetic, body(): totals.at[blocks[:, None], :, blocks[None, :], :]  60.2 us
    all_to_all x1, blocking collectives, copy_for_each(): return lax.all_to_all(copies, axis, split_axis=0, concat_axis=0, tiled=True)  55.2 us
    all_to_all x1, waiting for transfers between devices, copy_for_each(): return lax.all_to_all(copies, axis, split_axis=0, concat_axis=0, tiled=True)  41.9 us
  transfers between devices with their start and end apart: 6, of which 5 were waited for; matrix products, arithmetic and copies ran while one was open for 4% of the time, Pallas kernels for 0%

commit v1 on v0

v1 whole, which is shorter than its diff:
```python
import jax
import jax.numpy as jnp
from jax import lax
from jax.experimental import pallas as pl
from jax.experimental.pallas import tpu as pltpu
from jax.sharding import PartitionSpec as P

MESH = pl.DeviceIdType.MESH
NX = 4
NY = 4
NZ = 8
NCHIP = NX * NY
BF16 = jnp.bfloat16
F32 = jnp.float32
NT = (((1,), (1,)), ((), ()))
TN = (((0,), (0,)), ((), ()))


def mod(a, n):
    return lax.rem(a, n)


def kernel(
    sel, inv, dens, xin, pts, wts, out,
    pg, xg, psel, fs, fr, mg, pot, xd, kc, kp, d0, s1, rb, cb, t1, rb2, cb2, z1, zr,
    x_s, x_r, p_s, p_r, q_s, q_r, f_s, f_r, m_s, m_r, d_s, d_r, a_s, a_r, b_s, b_r, z_s, z_r,
):
    g = lax.axis_index("grid")
    r = lax.axis_index("rows")
    core = mod(g, 2)
    chip = lax.div(g, 2)
    x = mod(chip, NX)
    y = lax.div(chip, NX)

    def at_plane(xx, yy):
        return (2 * (NX * yy + xx) + core, r)

    def at_z(rr):
        return (g, rr)

    partner = (2 * chip + 1 - core, r)

    def remote(src, dst, send, recv, device):
        return pltpu.make_async_remote_copy(
            src_ref=src, dst_ref=dst, send_sem=send, recv_sem=recv, device_id=device, device_id_type=MESH
        )

    bar = pltpu.get_barrier_semaphore()
    for k in range(1, NCHIP):
        device = at_plane(mod(x + k % NX, NX), mod(y + k // NX, NY))
        pl.semaphore_signal(bar, inc=1, device_id=device, device_id_type=MESH)
    for k in range(1, NZ):
        pl.semaphore_signal(bar, inc=1, device_id=at_z(mod(r + k, NZ)), device_id_type=MESH)
    pl.semaphore_signal(bar, inc=1, device_id=partner, device_id_type=MESH)
    pl.semaphore_wait(bar, NCHIP - 1 + NZ - 1 + 1)

    up, down = at_z(mod(r + 1, NZ)), at_z(mod(r + NZ - 1, NZ))

    def shard_of(d, t):
        return mod(r + (NZ - t if d == 0 else t), NZ)

    def x_copy(d, t, b):
        dst = xg.at[b, pl.ds(0, 16), shard_of(d, t)]
        src = xin.at[b] if t == 0 else dst
        return remote(src, dst, x_s.at[d, t, b], x_r.at[d, t, b], up if d == 0 else down)

    ring = [(d, t, b) for t in range(4) for b in range(2) for d in range(2) if t < 3 or b == d]

    def p_copy(k):
        device = at_plane(mod(x + mod(k, NX), NX), mod(y + lax.div(k, NX), NY))
        return remote(dens, pg.at[g], p_s.at[k], p_r.at[k], device)

    def p_forward(k):
        xs, ys = mod(x + NX - mod(k, NX), NX), mod(y + NY - lax.div(k, NX), NY)
        slot = 2 * (NX * ys + xs) + core
        src = dens if isinstance(k, int) else pg.at[slot]
        return remote(src, pg.at[slot], q_s.at[k], q_r.at[k], partner)

    for d, t, b in ring[:4]:
        x_copy(d, t, b).start()

    @pl.loop(1, NCHIP)
    def _(k):
        p_copy(k).start()

    pg[g] = dens[...]
    for b in range(2):
        xg[b, 0:16, r] = xin[b]
        xg[b, 16] = jnp.zeros(xg.shape[2:], BF16)
        kc[b, 16] = jnp.zeros(kc.shape[2:], F32)

    def x_step(t):
        for d, tt, b in ring:
            if tt == t:
                x_copy(d, t - 1, b).wait_recv()
                x_copy(d, t, b).start()

    x_step(1)
    x_step(2)

    p_forward(0).start()

    @pl.loop(1, NCHIP)
    def _(k):
        p_copy(k).wait_recv()
        p_forward(k).start()

    x_step(3)

    @pl.loop(0, NCHIP)
    def _(k):
        p_forward(k).wait_recv()

    @pl.loop(0, 16)
    def _(s):
        for b in range(2):
            row = sel[b, s]
            for c in range(16):
                psel[b, s, :, 128 * c : 128 * (c + 1)] = pg[sel[b, c], row]

    for d, t, b in ring:
        if t == 3 or (t == 2 and b != d):
            x_copy(d, t, b).wait_recv()

    for b in range(2):
        rows = psel[b].reshape(256, 2048)
        for h in range(2):
            f = jnp.dot(
                rows, xg[b, 0:16, :, :, 256 * h : 256 * (h + 1)].reshape(2048, 256), preferred_element_type=F32
            ).astype(BF16)
            fs[b, 2 * h] = f[:, 0:128].reshape(16, 16, 128)
            fs[b, 2 * h + 1] = f[:, 128:256].reshape(16, 16, 128)

    def f_copy(k):
        to = mod(r + k, NZ)
        return remote(fs.at[lax.div(to, 4), mod(to, 4)], fr.at[:, r], f_s.at[k], f_r.at[k], at_z(to))

    for k in (4, 3, 5, 2, 6, 1, 7):
        f_copy(k).start()
    my_b, my_q = lax.div(r, 4), mod(r, 4)
    fr[:, r] = fs[my_b, my_q]

    lanes = pl.ds(pl.multiple_of(128 * my_q, 128), 128)
    dist = jnp.zeros((128, 512), F32)
    for c in range(3):
        across = pts[my_b, c : c + 1, :]
        down_col = jnp.broadcast_to(pts[my_b, c : c + 1, lanes], (128, 128)).T
        diff = across - jnp.concatenate([down_col] * 4, axis=1)
        dist = dist + diff * diff
    scale = wts[my_b] * (1.0 / jnp.sqrt(dist + 0.5))

    for k in range(1, NZ):
        f_copy(k).wait_recv()
    inter = lax.dot_general(
        fr[...].reshape(2048, 128), xg[my_b, 0:16].reshape(2048, 512), TN, preferred_element_type=F32
    )
    mg[r] = (scale * inter).astype(BF16)

    def m_copy(d, t, h):
        ref = mg.at[shard_of(d, t), pl.ds(64 * h, 64)]
        return remote(ref, ref, m_s.at[d, t, h], m_r.at[d, t, h], up if d == 0 else down)

    for d, t, h in ring[:4]:
        m_copy(d, t, h).start()
    for d, t, h in ring[4:]:
        m_copy(d, t - 1, h).wait_recv()
        m_copy(d, t, h).start()
    for d, t, h in ring:
        if t == 3 or (t == 2 and h != d):
            m_copy(d, t, h).wait_recv()

    for b in range(2):
        m = mg[4 * b : 4 * b + 4].reshape(512, 512)
        full = lax.dot_general(xin[b].reshape(256, 512), m, NT, preferred_element_type=F32)
        pot[b] = (full * wts[b]).astype(BF16)

    def d_copy(rp):
        return remote(kp.at[1 - core, rp], d0.at[rp], d_s.at[rp], d_r.at[rp], partner)

    @pl.loop(0, 4)
    def _(p):
        for half in range(2):
            rp = p + 4 * half
            for b in range(2):
                for a in range(32):
                    xd[b, a] = xg[b, inv[b, a], rp]
                kc[b, 0:16] = lax.dot_general(
                    pot[b], xd[b].reshape(512, 512), NT, preferred_element_type=F32
                ).reshape(16, 16, 512)
            for v in range(4):
                for u in range(4):
                    for c in range(2):
                        nb = 2 * (NX * v + u if half == 0 else NX * u + v) + c
                        kp[c, rp, v, u] = kc[0, inv[0, nb]] + kc[1, inv[1, nb]]
            d_copy(rp).start()

    first = (x, y)
    second = (y, x)
    low, high = pl.ds(0, 8), pl.ds(8, 8)

    def along(half, stage, shift):
        if half == stage:
            return at_plane(mod(x + shift, NX), y)
        return at_plane(x, mod(y + shift, NY))

    def a_copy(half, rp, m):
        u = first[half]
        nxt, opp, prv = mod(u + 1, 4), mod(u + 2, 4), mod(u + 3, 4)
        src = (
            s1.at[rp, :, opp, low], s1.at[rp, :, nxt, high], cb.at[0, rp],
            s1.at[rp, :, opp, high], s1.at[rp, :, prv, low], cb.at[1, rp],
        )[m]
        return remote(src, rb.at[m, rp], a_s.at[m, rp], a_r.at[m, rp], along(half, 0, 1 if m < 3 else 3))

    def b_copy(half, rp, m):
        u = second[half]
        nxt, opp, prv = mod(u + 1, 4), mod(u + 2, 4), mod(u + 3, 4)
        src = (
            t1.at[rp, opp, low], t1.at[rp, nxt, high], cb2.at[0, rp],
            t1.at[rp, opp, high], t1.at[rp, prv, low], cb2.at[1, rp],
        )[m]
        return remote(src, rb2.at[m, rp], b_s.at[m, rp], b_r.at[m, rp], along(half, 1, 1 if m < 3 else 3))

    @pl.loop(0, 4)
    def _(p):
        for half in range(2):
            rp = p + 4 * half
            d_copy(rp).wait_recv()
            s1[rp] = kp[core, rp] + d0[rp]
            for m in (0, 3, 1, 4):
                a_copy(half, rp, m).start()

    @pl.loop(0, 4)
    def _(p):
        for half in range(2):
            rp = p + 4 * half
            u = first[half]
            a_copy(half, rp, 0).wait_recv()
            cb[0, rp] = rb[0, rp] + s1[rp, :, mod(u + 1, 4), 0:8]
            a_copy(half, rp, 2).start()
            a_copy(half, rp, 3).wait_recv()
            cb[1, rp] = rb[3, rp] + s1[rp, :, mod(u + 3, 4), 8:16]
            a_copy(half, rp, 5).start()

    @pl.loop(0, 4)
    def _(p):
        for half in range(2):
            rp = p + 4 * half
            u = first[half]
            for m in (1, 4, 2, 5):
                a_copy(half, rp, m).wait_recv()
            t1[rp, :, 0:8] = s1[rp, :, u, 0:8] + rb[4, rp] + rb[2, rp]
            t1[rp, :, 8:16] = s1[rp, :, u, 8:16] + rb[1, rp] + rb[5, rp]
            for m in (0, 3, 1, 4):
                b_copy(half, rp, m).start()

    @pl.loop(0, 4)
    def _(p):
        for half in range(2):
            rp = p + 4 * half
            u = second[half]
            b_copy(half, rp, 0).wait_recv()
            cb2[0, rp] = rb2[0, rp] + t1[rp, mod(u + 1, 4), 0:8]
            b_copy(half, rp, 2).start()
            b_copy(half, rp, 3).wait_recv()
            cb2[1, rp] = rb2[3, rp] + t1[rp, mod(u + 3, 4), 8:16]
            b_copy(half, rp, 5).start()

    def z_copy(rp):
        return remote(z1.at[rp], zr.at[r], z_s.at[rp], z_r.at[r], at_z(rp))

    @pl.loop(0, 4)
    def _(p):
        for half in range(2):
            rp = p + 4 * half
            u = second[half]
            for m in (1, 4, 2, 5):
                b_copy(half, rp, m).wait_recv()
            z1[rp, 0:8] = t1[rp, u, 0:8] + rb2[4, rp] + rb2[2, rp]
            z1[rp, 8:16] = t1[rp, u, 8:16] + rb2[1, rp] + rb2[5, rp]

            @pl.when(rp != r)
            def _():
                z_copy(rp).start()

    zr[r] = z1[r]

    @pl.loop(1, NZ)
    def _(k):
        source = mod(r + k, NZ)
        remote(z1.at[source], zr.at[source], z_s.at[source], z_r.at[source], at_z(source)).wait_recv()

    for c in range(4):
        block = zr[:, :, 128 * c : 128 * (c + 1)].reshape(128, 128)
        out[8 * c : 8 * c + 8] = block.T.reshape(8, 16, 128)

    for d, t, b in ring:
        x_copy(d, t, b).wait_send()
        m_copy(d, t, b).wait_send()

    p_forward(0).wait_send()

    @pl.loop(1, NCHIP)
    def _(k):
        p_copy(k).wait_send()
        p_forward(k).wait_send()

    @pl.loop(1, NZ)
    def _(k):
        f_copy(k).wait_send()
        z_copy(mod(r + k, NZ)).wait_send()

    @pl.loop(0, 4)
    def _(p):
        for half in range(2):
            rp = p + 4 * half
            d_copy(rp).wait_send()
            for m in range(6):
                a_copy(half, rp, m).wait_send()
                b_copy(half, rp, m).wait_send()


def body(density, basis_values, grid_points, grid_weights, screened_blocks):
    wanted = jnp.arange(32, dtype=jnp.int32)
    hits = screened_blocks[:, :, None] == wanted[None, None, :]
    inverse = jnp.min(jnp.where(hits, jnp.arange(16, dtype=jnp.int32)[None, :, None], 16), axis=1)
    vmem = pl.BlockSpec(memory_space=pltpu.VMEM)
    smem = pl.BlockSpec(memory_space=pltpu.SMEM)
    dma = pltpu.SemaphoreType.DMA
    return pl.pallas_call(
        kernel,
        out_shape=jax.ShapeDtypeStruct((32, 16, 128), F32),
        in_specs=[smem, smem, vmem, vmem, vmem, vmem],
        out_specs=vmem,
        scratch_shapes=[
            pltpu.VMEM((32, 32, 16, 128), BF16),
            pltpu.VMEM((2, 17, 8, 16, 512), BF16),
            pltpu.VMEM((2, 16, 16, 2048), BF16),
            pltpu.VMEM((2, 4, 16, 16, 128), BF16),
            pltpu.VMEM((16, 8, 16, 128), BF16),
            pltpu.VMEM((8, 128, 512), BF16),
            pltpu.VMEM((2, 256, 512), BF16),
            pltpu.VMEM((2, 32, 16, 512), BF16),
            pltpu.VMEM((2, 17, 16, 512), F32),
            pltpu.VMEM((2, 8, 4, 4, 16, 512), F32),
            pltpu.VMEM((8, 4, 4, 16, 512), F32),
            pltpu.VMEM((8, 4, 4, 16, 512), F32),
            pltpu.VMEM((6, 8, 4, 8, 512), F32),
            pltpu.VMEM((2, 8, 4, 8, 512), F32),
            pltpu.VMEM((8, 4, 16, 512), F32),
            pltpu.VMEM((6, 8, 8, 512), F32),
            pltpu.VMEM((2, 8, 8, 512), F32),
            pltpu.VMEM((8, 16, 512), F32),
            pltpu.VMEM((8, 16, 512), F32),
            dma((2, 4, 2)), dma((2, 4, 2)),
            dma((16,)), dma((16,)),
            dma((16,)), dma((16,)),
            dma((8,)), dma((8,)),
            dma((2, 4, 2)), dma((2, 4, 2)),
            dma((8,)), dma((8,)),
            dma((6, 8)), dma((6, 8)),
            dma((6, 8)), dma((6, 8)),
            dma((8,)), dma((8,)),
        ],
        compiler_params=pltpu.CompilerParams(
            collective_id=0, has_side_effects=True, vmem_limit_bytes=60 * 1024 * 1024
        ),
        cost_estimate=pl.CostEstimate(flops=4_000_000_000, bytes_accessed=2_000_000, transcendentals=100_000),
        name="exchange",
    )(screened_blocks, inverse, density, basis_values, grid_points, grid_weights[:, None, :])


def solution(mesh):
    placed = (
        P(None, "rows", "grid"),
        P("grid", None, "rows", None),
        P("grid", None, None),
        P("grid", None),
        P("grid", None),
    )
    return jax.shard_map(
        body, mesh=mesh, in_specs=placed, out_specs=P(None, "rows", "grid"), check_vma=False
    )
```

time: 496 us -> 127 us (0.26)
  waiting for transfers between devices: 295 us -> 0 us
  Pallas kernels: 0 us -> 120 us
  other arithmetic: 61.5 us -> 1.34 us
  blocking collectives: 55.2 us -> 0 us
  local copies, waits for them, and re-layouts: 43.8 us -> 4.26 us
  matrix products: 17.9 us -> 0 us
  between operations: 13.4 us -> 0.01 us
  starting transfers between devices: 7.56 us -> 0 us
    pallas_call x0 -> x1, Pallas kernels: none -> 120 us  [body(): pl.pallas_call(kernel, out_shape=jax.ShapeDtypeStruct((32, 16, 128), F32)...]
    reduce_scatter x1 -> x0, waiting for transfers between devices: 99.9 us -> none  [body(): lax.psum_scatter(totals.reshape(nblocks, rows_mine, nbasis), 'grid', scat...]
    psum x1 -> x0, waiting for transfers between devices: 80.8 us -> none  [body(): intersection = lax.psum(intersection_part, 'rows')]
    all_gather x3 -> x0, waiting for transfers between devices: 71.2 us -> none  [the longest x2 71.2 us: body(): lax.all_gather(potential, 'rows', axis=1, tiled=True)]
    scatter-add x2 -> x0, other arithmetic: 60.2 us -> none  [body(): totals.at[blocks[:, None], :, blocks[None, :], :]]
    all_to_all x1 -> x0, blocking collectives: 55.2 us -> none  [copy_for_each(): return lax.all_to_all(copies, axis, split_axis=0, concat_axis=0, tiled=True)]
    all_to_all x1 -> x0, waiting for transfers between devices: 41.9 us -> none  [copy_for_each(): return lax.all_to_all(copies, axis, split_axis=0, concat_axis=0, tiled=True)]
    dot_general x6 -> x0, matrix products: 17.9 us -> none  [the longest x2 7.34 us: body(): lax.dot_general(x_mine, fmat, (((0,), (0,)), ((), ())), preferred_element...]
  transfers between devices with their start and end apart: 6 -> 0, of which waited for: 5 -> 0; matrix products, arithmetic and copies ran while one was open for 4% -> 0% of each run, Pallas kernels for 0% -> 0%
where the time goes in v1:
time: 127 us; the launch traced here: 126 us
  Pallas kernels  120 us (94%)
  local copies, waits for them, and re-layouts  4.26 us (3%)
  other arithmetic  1.34 us (1%)
    pallas_call x1, Pallas kernels, body(): pl.pallas_call(kernel, out_shape=jax.ShapeDtypeStruct((32, 16, 128), F32)...  120 us
    unnamed x2, local copies, waits for them, and re-layouts  2.99 us

profile of v1, /device:TPU:96, one launch (start us, length us, event | category | flops | bytes accessed | tf_op | source)
XLA Modules:
  0.0 126.0 jit_solution(17735125423257818762)
XLA Ops:
  0.0 1.3 %select_reduce_fusion.inv = s32[2,32]{1,0:T(2,128)} fusion(s32[2,16]{1,0:T(2,128)} %sel.1), kind=kLoop, calls=%fused_computation | loop fusion | flops 3008 | bytes 384 | tf_op jit(solution)/shard_map/reduce_min | solution.py:326
  1.3 1.3 %broadcast_in_dim.20.wts = f32[2,1,512]{2,1,0:T(1,128)} reshape(f32[2,512]{1,0:T(2,128)} %param.8) | data formatting | bytes 8192 | tf_op jit(solution)/shard_map/broadcast_in_dim | solution.py:370
  2.6 1.3 %copy.7.pts = f32[2,3,512]{2,1,0:T(4,128)} copy(f32[2,3,512]{2,0,1:T(2,128)} %param.7) | data formatting | bytes 24576 | tf_op args[2]
  3.9 120.4 %exchange.1 = f32[32,16,128]{2,1,0:T(8,128)} custom-call(s32[2,16]{1,0:T(2,128)} %sel.1, s32[2,32]{1,0:T(2,128)} %select_reduce_fusion.inv, bf16[32,16,128]{2,1,0:T(8,128)(2,1)} %dens.1, bf16[2,16,16,512]{3,2,1,0:T(8,128)(2,1)} %xin.1, f32[2,3,512]{2,1,0:T(4,128)} %copy.7.pts, f32[2,1,512]{2,1,0:T(1,128)} %broadcast_in_dim.20.wts), custom_call_target="tpu_custom_call" | custom-call | flops 4000000000 | bytes 2000000 | tf_op jit(solution)/shard_map/exchange/pallas_call | solution.py:330
  124.3 1.7 %copy.9 = f32[32,16,128]{2,1,0:T(8,128)} copy(f32[32,16,128]{2,1,0:T(8,128)} %exchange.1) | data formatting | bytes 524288

commit v2 on v1

v2 whole, which is shorter than its diff:
```python
import jax
import jax.numpy as jnp
from jax import lax
from jax.experimental import pallas as pl
from jax.experimental.pallas import tpu as pltpu
from jax.sharding import PartitionSpec as P

MESH = pl.DeviceIdType.MESH
NX = 4
NY = 4
NZ = 8
BF16 = jnp.bfloat16
F32 = jnp.float32
NT = (((1,), (1,)), ((), ()))
FAR_FIRST = (4, 3, 5, 2, 6, 1, 7)


def mod(a, n):
    return lax.rem(a, n)


def kernel(
    sel, dens, xin, pts, wts, out,
    inv, pg, xg, psel, tcol, scale, wcol, fs, fr, ps, pr, pot, xd, kc, kp, d0, s1, rb, cb, t1, rb2, cb2, z1, zr,
    x_s, x_r, p_s, p_r, q_s, q_r, f_s, f_r, m_s, m_r, d_s, d_r, a_s, a_r, b_s, b_r, z_s, z_r,
):
    g = lax.axis_index("grid")
    r = lax.axis_index("rows")
    core = mod(g, 2)
    chip = lax.div(g, 2)
    x = mod(chip, NX)
    y = lax.div(chip, NX)
    finish = []

    def at_plane(xx, yy):
        return (2 * (NX * yy + xx) + core, r)

    def at_z(rr):
        return (g, rr)

    partner = (2 * chip + 1 - core, r)
    up, down = at_z(mod(r + 1, NZ)), at_z(mod(r + NZ - 1, NZ))
    east, west = at_plane(mod(x + 1, NX), y), at_plane(mod(x + NX - 1, NX), y)
    north, south = at_plane(x, mod(y + 1, NY)), at_plane(x, mod(y + NY - 1, NY))

    def remote(src, dst, send, recv, device):
        return pltpu.make_async_remote_copy(
            src_ref=src, dst_ref=dst, send_sem=send, recv_sem=recv, device_id=device, device_id_type=MESH
        )

    bar = pltpu.get_barrier_semaphore()
    for device in (up, down, east, west, north, south, partner):
        pl.semaphore_signal(bar, inc=1, device_id=device, device_id_type=MESH)
    pl.semaphore_wait(bar, 7)

    def x_copy(d, t, b):
        shard = mod(r + (NZ - t if d == 0 else t), NZ)
        part = pl.ds(0, 16) if t < 3 else pl.ds(8 * d, 8)
        dst = xg.at[b, part, shard]
        src = xin.at[b] if t == 0 else dst
        return remote(src, dst, x_s.at[d, t, b], x_r.at[d, t, b], up if d == 0 else down)

    def x_send(t, b):
        for d in range(2):
            if t > 0:
                x_copy(d, t - 1, b).wait_recv()
            x_copy(d, t, b).start()

    def px_copy(d, t):
        if t == 0:
            src, dst = dens, pg.at[y, x, core]
        else:
            dst = pg.at[y, mod(x + (3 if d == 0 else 1), NX), core, pl.ds(16 * d, 16)]
            src = dst
        return remote(src, dst, p_s.at[0, d, t], p_r.at[0, d, t], east if d == 0 else west)

    def py_copy(d, t):
        if t == 0:
            ref = pg.at[y, :, core]
        else:
            ref = pg.at[mod(y + (3 if d == 0 else 1), NY), :, core, pl.ds(16 * d, 16)]
        return remote(ref, ref, p_s.at[1, d, t], p_r.at[1, d, t], north if d == 0 else south)

    def pq_copy(k):
        ref = pg.at[mod(y + k, NY), :, core]
        return remote(ref, ref, q_s.at[k], q_r.at[k], partner)

    x_send(0, 0)
    px_copy(0, 0).start()
    px_copy(1, 0).start()
    x_send(0, 1)

    pg[y, x, core] = dens[...]
    for b in range(2):
        xg[b, 0:16, r] = xin[b]
        xg[b, 16] = jnp.zeros(xg.shape[2:], BF16)
        kc[b, 16] = jnp.zeros(kc.shape[2:], F32)

    px_copy(0, 0).wait_recv()
    px_copy(0, 1).start()
    px_copy(1, 0).wait_recv()
    px_copy(1, 1).start()

    @pl.loop(0, 32)
    def _(nb):
        for b in range(2):
            at = jnp.int32(16)
            for s in range(16):
                at = jnp.where(sel[b, s] == nb, s, at)
            inv[b, nb] = at

    x_send(1, 0)

    px_copy(0, 1).wait_recv()
    px_copy(1, 1).wait_recv()
    py_copy(0, 0).start()
    py_copy(1, 0).start()
    pq_copy(0).start()

    lanes = pl.ds(pl.multiple_of(128 * lax.div(r, 2), 128), 128)
    mine = pl.ds(pl.multiple_of(64 * mod(r, 2), 64), 64)
    for b in range(2):
        for c in range(4):
            row = pts[c, b : b + 1, lanes] if c < 3 else wts[b : b + 1, lanes]
            tcol[b, c] = jnp.broadcast_to(row, (128, 128)).T
        dist = jnp.zeros((64, 512), F32)
        for c in range(3):
            diff = pts[c, b : b + 1, :] - jnp.concatenate([tcol[b, c, mine]] * 4, axis=1)
            dist = dist + diff * diff
        scale[b] = wts[b : b + 1, :] * (1.0 / jnp.sqrt(dist + 0.5))
        wcol[b] = tcol[b, 3, mine]

    x_send(1, 1)
    x_send(2, 0)

    for d in range(2):
        py_copy(d, 0).wait_recv()
        py_copy(d, 1).start()
    pq_copy(1).start()
    pq_copy(3).start()

    x_send(2, 1)
    x_send(3, 0)

    py_copy(0, 1).wait_recv()
    py_copy(1, 1).wait_recv()
    pq_copy(2).start()

    x_send(3, 1)

    for k in range(4):
        pq_copy(k).wait_recv()

    def finish_gathers():
        for d in range(2):
            for t in range(4):
                for b in range(2):
                    x_copy(d, t, b).wait_send()
            for t in range(2):
                px_copy(d, t).wait_send()
                py_copy(d, t).wait_send()
        for k in range(4):
            pq_copy(k).wait_send()

    finish.append(finish_gathers)

    @pl.loop(0, 16)
    def _(s):
        for b in range(2):
            row = sel[b, s]
            for c in range(16):
                col = sel[b, c]
                psel[b, s, :, 128 * c : 128 * (c + 1)] = pg[
                    lax.div(col, 8), mod(lax.div(col, 2), 4), mod(col, 2), row
                ]

    def f_copy(b, k):
        to = mod(r + k, NZ)
        return remote(fs.at[b, to], fr.at[b, r], f_s.at[b, k], f_r.at[b, k], at_z(to))

    for b in range(2):
        for d in range(2):
            x_copy(d, 3, b).wait_recv()
        f = jnp.dot(
            psel[b].reshape(256, 2048), xg[b, 0:16].reshape(2048, 512), preferred_element_type=F32
        ).astype(BF16)
        fs[b] = f.T.reshape(8, 64, 256)
        for k in FAR_FIRST:
            f_copy(b, k).start()
        fr[b, r] = fs[b, r]

    def finish_f():
        for b in range(2):
            for k in FAR_FIRST:
                f_copy(b, k).wait_send()

    finish.append(finish_f)

    def m_copy(b, k):
        to = mod(r + k, NZ)
        return remote(ps.at[b, to], pr.at[b, r], m_s.at[b, k], m_r.at[b, k], at_z(to))

    for b in range(2):
        for k in FAR_FIRST:
            f_copy(b, k).wait_recv()
        inter = jnp.zeros((64, 512), F32)
        for s in range(8):
            inter = inter + jnp.dot(fr[b, s], xg[b, 0:16, s].reshape(256, 512), preferred_element_type=F32)
        mixed = (scale[b] * inter).astype(BF16)
        factor = jnp.concatenate([wcol[b]] * 2, axis=1)
        for s in range(8):
            p = lax.dot_general(mixed, xg[b, 0:16, s].reshape(256, 512), NT, preferred_element_type=F32)
            ps[b, s] = (p * factor).astype(BF16)
        for k in FAR_FIRST:
            m_copy(b, k).start()
        pr[b, r] = ps[b, r]

    def finish_m():
        for b in range(2):
            for k in FAR_FIRST:
                m_copy(b, k).wait_send()

    finish.append(finish_m)

    for b in range(2):
        for k in FAR_FIRST:
            m_copy(b, k).wait_recv()
        pot[b] = pr[b].reshape(512, 256).T

    first = (x, y)
    second = (y, x)
    low, high = pl.ds(0, 8), pl.ds(8, 8)

    def d_copy(rp):
        return remote(kp.at[1 - core, rp], d0.at[rp], d_s.at[rp], d_r.at[rp], partner)

    def along(half, stage, shift):
        if half == stage:
            return at_plane(mod(x + shift, NX), y)
        return at_plane(x, mod(y + shift, NY))

    def a_copy(half, rp, m):
        u = first[half]
        nxt, opp, prv = mod(u + 1, 4), mod(u + 2, 4), mod(u + 3, 4)
        src = (
            s1.at[rp, :, opp, low], s1.at[rp, :, nxt, high], cb.at[0, rp],
            s1.at[rp, :, opp, high], s1.at[rp, :, prv, low], cb.at[1, rp],
        )[m]
        return remote(src, rb.at[m, rp], a_s.at[m, rp], a_r.at[m, rp], along(half, 0, 1 if m < 3 else 3))

    def b_copy(half, rp, m):
        u = second[half]
        nxt, opp, prv = mod(u + 1, 4), mod(u + 2, 4), mod(u + 3, 4)
        src = (
            t1.at[rp, opp, low], t1.at[rp, nxt, high], cb2.at[0, rp],
            t1.at[rp, opp, high], t1.at[rp, prv, low], cb2.at[1, rp],
        )[m]
        return remote(src, rb2.at[m, rp], b_s.at[m, rp], b_r.at[m, rp], along(half, 1, 1 if m < 3 else 3))

    def make_slice(half, rp):
        for b in range(2):
            for a in range(32):
                xd[b, a] = xg[b, inv[b, a], rp]
            kc[b, 0:16] = lax.dot_general(
                pot[b], xd[b].reshape(512, 512), NT, preferred_element_type=F32
            ).reshape(16, 16, 512)
        for v in range(4):
            for u in range(4):
                for c in range(2):
                    nb = 2 * (NX * v + u if half == 0 else NX * u + v) + c
                    kp[c, rp, v, u] = kc[0, inv[0, nb]] + kc[1, inv[1, nb]]
        d_copy(rp).start()

    def send_slice(half, rp):
        d_copy(rp).wait_recv()
        s1[rp] = kp[core, rp] + d0[rp]
        for m in (0, 3, 1, 4):
            a_copy(half, rp, m).start()

    def finish_a():
        @pl.loop(0, 4)
        def _(p):
            for half in range(2):
                d_copy(p + 4 * half).wait_send()
                for m in range(6):
                    a_copy(half, p + 4 * half, m).wait_send()

    finish.append(finish_a)

    @pl.loop(0, 4)
    def _(p):
        for half in range(2):
            make_slice(half, p + 4 * half)

            @pl.when(p > 0)
            def _():
                send_slice(half, p + 4 * half - 1)

    for half in range(2):
        send_slice(half, 3 + 4 * half)


    @pl.loop(0, 4)
    def _(p):
        for half in range(2):
            rp = p + 4 * half
            u = first[half]
            a_copy(half, rp, 0).wait_recv()
            cb[0, rp] = rb[0, rp] + s1[rp, :, mod(u + 1, 4), 0:8]
            a_copy(half, rp, 2).start()
            a_copy(half, rp, 3).wait_recv()
            cb[1, rp] = rb[3, rp] + s1[rp, :, mod(u + 3, 4), 8:16]
            a_copy(half, rp, 5).start()

    @pl.loop(0, 4)
    def _(p):
        for half in range(2):
            rp = p + 4 * half
            u = first[half]
            for m in (1, 4, 2, 5):
                a_copy(half, rp, m).wait_recv()
            t1[rp, :, 0:8] = s1[rp, :, u, 0:8] + rb[4, rp] + rb[2, rp]
            t1[rp, :, 8:16] = s1[rp, :, u, 8:16] + rb[1, rp] + rb[5, rp]
            for m in (0, 3, 1, 4):
                b_copy(half, rp, m).start()

    @pl.loop(0, 4)
    def _(p):
        for half in range(2):
            rp = p + 4 * half
            u = second[half]
            b_copy(half, rp, 0).wait_recv()
            cb2[0, rp] = rb2[0, rp] + t1[rp, mod(u + 1, 4), 0:8]
            b_copy(half, rp, 2).start()
            b_copy(half, rp, 3).wait_recv()
            cb2[1, rp] = rb2[3, rp] + t1[rp, mod(u + 3, 4), 8:16]
            b_copy(half, rp, 5).start()

    def z_copy(rp):
        return remote(z1.at[rp], zr.at[r], z_s.at[rp], z_r.at[r], at_z(rp))

    @pl.loop(0, 4)
    def _(p):
        for half in range(2):
            rp = p + 4 * half
            u = second[half]
            for m in (1, 4, 2, 5):
                b_copy(half, rp, m).wait_recv()
            z1[rp, 0:8] = t1[rp, u, 0:8] + rb2[4, rp] + rb2[2, rp]
            z1[rp, 8:16] = t1[rp, u, 8:16] + rb2[1, rp] + rb2[5, rp]

            @pl.when(rp != r)
            def _():
                z_copy(rp).start()

    zr[r] = z1[r]

    @pl.loop(1, NZ)
    def _(k):
        source = mod(r + k, NZ)
        remote(z1.at[source], zr.at[source], z_s.at[source], z_r.at[source], at_z(source)).wait_recv()

    for c in range(4):
        block = zr[:, :, 128 * c : 128 * (c + 1)].reshape(128, 128)
        out[8 * c : 8 * c + 8] = block.T.reshape(8, 16, 128)

    for waits in finish:
        waits()

    @pl.loop(0, 4)
    def _(p):
        for half in range(2):
            for m in range(6):
                b_copy(half, p + 4 * half, m).wait_send()

    @pl.loop(1, NZ)
    def _(k):
        z_copy(mod(r + k, NZ)).wait_send()


def body(density, basis_values, grid_points, grid_weights, screened_blocks):
    vmem = pl.BlockSpec(memory_space=pltpu.VMEM)
    smem = pl.BlockSpec(memory_space=pltpu.SMEM)
    dma = pltpu.SemaphoreType.DMA
    return pl.pallas_call(
        kernel,
        out_shape=jax.ShapeDtypeStruct((32, 16, 128), F32),
        in_specs=[smem, vmem, vmem, vmem, vmem],
        out_specs=vmem,
        scratch_shapes=[
            pltpu.SMEM((2, 32), jnp.int32),
            pltpu.VMEM((4, 4, 2, 32, 16, 128), BF16),
            pltpu.VMEM((2, 17, 8, 16, 512), BF16),
            pltpu.VMEM((2, 16, 16, 2048), BF16),
            pltpu.VMEM((2, 4, 128, 128), F32),
            pltpu.VMEM((2, 64, 512), F32),
            pltpu.VMEM((2, 64, 128), F32),
            pltpu.VMEM((2, 8, 64, 256), BF16),
            pltpu.VMEM((2, 8, 64, 256), BF16),
            pltpu.VMEM((2, 8, 64, 256), BF16),
            pltpu.VMEM((2, 8, 64, 256), BF16),
            pltpu.VMEM((2, 256, 512), BF16),
            pltpu.VMEM((2, 32, 16, 512), BF16),
            pltpu.VMEM((2, 17, 16, 512), F32),
            pltpu.VMEM((2, 8, 4, 4, 16, 512), F32),
            pltpu.VMEM((8, 4, 4, 16, 512), F32),
            pltpu.VMEM((8, 4, 4, 16, 512), F32),
            pltpu.VMEM((6, 8, 4, 8, 512), F32),
            pltpu.VMEM((2, 8, 4, 8, 512), F32),
            pltpu.VMEM((8, 4, 16, 512), F32),
            pltpu.VMEM((6, 8, 8, 512), F32),
            pltpu.VMEM((2, 8, 8, 512), F32),
            pltpu.VMEM((8, 16, 512), F32),
            pltpu.VMEM((8, 16, 512), F32),
            dma((2, 4, 2)), dma((2, 4, 2)),
            dma((2, 2, 2)), dma((2, 2, 2)),
            dma((4,)), dma((4,)),
            dma((2, 8)), dma((2, 8)),
            dma((2, 8)), dma((2, 8)),
            dma((8,)), dma((8,)),
            dma((6, 8)), dma((6, 8)),
            dma((6, 8)), dma((6, 8)),
            dma((8,)), dma((8,)),
        ],
        compiler_params=pltpu.CompilerParams(
            collective_id=0, has_side_effects=True, vmem_limit_bytes=60 * 1024 * 1024
        ),
        cost_estimate=pl.CostEstimate(flops=4_000_000_000, bytes_accessed=2_000_000, transcendentals=100_000),
        name="exchange",
    )(screened_blocks, density, basis_values, jnp.transpose(grid_points, (1, 0, 2)), grid_weights)


def solution(mesh):
    placed = (
        P(None, "rows", "grid"),
        P("grid", None, "rows", None),
        P("grid", None, None),
        P("grid", None),
        P("grid", None),
    )
    return jax.shard_map(
        body, mesh=mesh, in_specs=placed, out_specs=P(None, "rows", "grid"), check_vma=False
    )
```

time: 127 us -> 113 us (0.89)
  Pallas kernels: 120 us -> 111 us
  local copies, waits for them, and re-layouts: 4.26 us -> 1.67 us
  other arithmetic: 1.34 us -> 0 us
    pallas_call x1, Pallas kernels: 120 us -> 111 us  [body(): pl.pallas_call(kernel, out_shape=jax.ShapeDtypeStruct((32, 16, 128), F32)...]
    reduce_min x1 -> x0, other arithmetic: 1.34 us -> none  [body(): jnp.min(jnp.where(hits, jnp.arange(16, dtype=jnp.int32)[None, :, None], 1...]
    unnamed x2 -> x1, local copies, waits for them, and re-layouts: 2.99 us -> 1.67 us
    broadcast_in_dim x1 -> x0, local copies, waits for them, and re-layouts: 1.28 us -> none  [body(): grid_weights[:, None, :]]
where the time goes in v2:
time: 113 us; the launch traced here: 112 us
  Pallas kernels  111 us (98%)
  local copies, waits for them, and re-layouts  1.67 us (1%)
    pallas_call x1, Pallas kernels, body(): pl.pallas_call(kernel, out_shape=jax.ShapeDtypeStruct((32, 16, 128), F32)...  111 us

profile of v2, /device:TPU:96, one launch (start us, length us, event | category | flops | bytes accessed | tf_op | source)
XLA Modules:
  0.0 112.3 jit_solution(15357882434707601714)
XLA Ops:
  0.0 110.7 %exchange.1 = f32[32,16,128]{2,1,0:T(8,128)} custom-call(s32[2,16]{1,0:T(2,128)} %sel.1, bf16[32,16,128]{2,1,0:T(8,128)(2,1)} %dens.1, bf16[2,16,16,512]{3,2,1,0:T(8,128)(2,1)} %xin.1, f32[3,2,512]{2,1,0:T(2,128)} %bitcast.1, f32[2,512]{1,0:T(2,128)} %wts.1), custom_call_target="tpu_custom_call" | custom-call | flops 4000000000 | bytes 2000000 | tf_op jit(solution)/shard_map/exchange/pallas_call | solution.py:385
  110.7 1.7 %copy.7 = f32[32,16,128]{2,1,0:T(8,128)} copy(f32[32,16,128]{2,1,0:T(8,128)} %exchange.1) | data formatting | bytes 524288

commit v3 on v2

--- a/solution.py
+++ b/solution.py
@@ -21,8 +21,8 @@
 
 def kernel(
     sel, dens, xin, pts, wts, out,
-    inv, pg, xg, psel, tcol, scale, wcol, fs, fr, ps, pr, pot, xd, kc, kp, d0, s1, rb, cb, t1, rb2, cb2, z1, zr,
-    x_s, x_r, p_s, p_r, q_s, q_r, f_s, f_r, m_s, m_r, d_s, d_r, a_s, a_r, b_s, b_r, z_s, z_r,
+    inv, pg, xg, psel, tcol, scale, wcol, fs, fr, ps, pr, pot, xd, k0, k1, kp, d0, s1, rb, cb, t1, rb2, z1,
+    o_s, x_s, x_r, p_s, p_r, q_s, q_r, f_s, f_r, m_s, m_r, d_s, d_r, a_s, a_r, b_s, b_r, z_s, z_r,
 ):
     g = lax.axis_index("grid")
     r = lax.axis_index("rows")
@@ -48,17 +48,21 @@
             src_ref=src, dst_ref=dst, send_sem=send, recv_sem=recv, device_id=device, device_id_type=MESH
         )
 
+    own = [pltpu.make_async_copy(xin.at[b], xg.at[b, pl.ds(0, 16), r], o_s.at[b]) for b in range(2)]
+    own.append(pltpu.make_async_copy(dens, pg.at[y, x, core], o_s.at[2]))
+    for copy in own:
+        copy.start()
     bar = pltpu.get_barrier_semaphore()
     for device in (up, down, east, west, north, south, partner):
         pl.semaphore_signal(bar, inc=1, device_id=device, device_id_type=MESH)
     pl.semaphore_wait(bar, 7)
+    own[0].wait()
 
     def x_copy(d, t, b):
         shard = mod(r + (NZ - t if d == 0 else t), NZ)
         part = pl.ds(0, 16) if t < 3 else pl.ds(8 * d, 8)
         dst = xg.at[b, part, shard]
-        src = xin.at[b] if t == 0 else dst
-        return remote(src, dst, x_s.at[d, t, b], x_r.at[d, t, b], up if d == 0 else down)
+        return remote(dst, dst, x_s.at[d, t, b], x_r.at[d, t, b], up if d == 0 else down)
 
     def x_send(t, b):
         for d in range(2):
@@ -68,11 +72,10 @@
 
     def px_copy(d, t):
         if t == 0:
-            src, dst = dens, pg.at[y, x, core]
+            ref = pg.at[y, x, core]
         else:
-            dst = pg.at[y, mod(x + (3 if d == 0 else 1), NX), core, pl.ds(16 * d, 16)]
-            src = dst
-        return remote(src, dst, p_s.at[0, d, t], p_r.at[0, d, t], east if d == 0 else west)
+            ref = pg.at[y, mod(x + (3 if d == 0 else 1), NX), core, pl.ds(16 * d, 16)]
+        return remote(ref, ref, p_s.at[0, d, t], p_r.at[0, d, t], east if d == 0 else west)
 
     def py_copy(d, t):
         if t == 0:
@@ -86,15 +89,18 @@
         return remote(ref, ref, q_s.at[k], q_r.at[k], partner)
 
     x_send(0, 0)
+    own[2].wait()
     px_copy(0, 0).start()
     px_copy(1, 0).start()
+    own[1].wait()
     x_send(0, 1)
 
-    pg[y, x, core] = dens[...]
+    for rp in range(8):
+        k0[rp, 16] = jnp.zeros(k0.shape[2:], F32)
+    for half in range(2):
+        k1[half, 16] = jnp.zeros(k1.shape[2:], F32)
     for b in range(2):
-        xg[b, 0:16, r] = xin[b]
         xg[b, 16] = jnp.zeros(xg.shape[2:], BF16)
-        kc[b, 16] = jnp.zeros(kc.shape[2:], F32)
 
     px_copy(0, 0).wait_recv()
     px_copy(0, 1).start()
@@ -222,17 +228,31 @@
 
     finish.append(finish_m)
 
-    for b in range(2):
+    def potential(b):
         for k in FAR_FIRST:
             m_copy(b, k).wait_recv()
         pot[b] = pr[b].reshape(512, 256).T
 
+    potential(0)
+
+    @pl.loop(0, 8)
+    def _(rp):
+        for a in range(32):
+            xd[8, a] = xg[0, inv[0, a], rp]
+        k0[rp, 0:16] = lax.dot_general(
+            pot[0], xd[8].reshape(512, 512), NT, preferred_element_type=F32
+        ).reshape(16, 16, 512)
+        for a in range(32):
+            xd[rp, a] = xg[1, inv[1, a], rp]
+
+    potential(1)
+
     first = (x, y)
     second = (y, x)
     low, high = pl.ds(0, 8), pl.ds(8, 8)
 
     def d_copy(rp):
-        return remote(kp.at[1 - core, rp], d0.at[rp], d_s.at[rp], d_r.at[rp], partner)
+        return remote(kp.at[rp], d0.at[rp], d_s.at[rp], d_r.at[rp], partner)
 
     def along(half, stage, shift):
         if half == stage:
@@ -249,31 +269,25 @@
         return remote(src, rb.at[m, rp], a_s.at[m, rp], a_r.at[m, rp], along(half, 0, 1 if m < 3 else 3))
 
     def b_copy(half, rp, m):
-        u = second[half]
-        nxt, opp, prv = mod(u + 1, 4), mod(u + 2, 4), mod(u + 3, 4)
-        src = (
-            t1.at[rp, opp, low], t1.at[rp, nxt, high], cb2.at[0, rp],
-            t1.at[rp, opp, high], t1.at[rp, prv, low], cb2.at[1, rp],
-        )[m]
-        return remote(src, rb2.at[m, rp], b_s.at[m, rp], b_r.at[m, rp], along(half, 1, 1 if m < 3 else 3))
+        shift = (2, 1, 3)[m]
+        src = t1.at[rp, mod(second[half] + shift, 4)]
+        return remote(src, rb2.at[m, rp], b_s.at[m, rp], b_r.at[m, rp], along(half, 1, shift))
 
     def make_slice(half, rp):
-        for b in range(2):
-            for a in range(32):
-                xd[b, a] = xg[b, inv[b, a], rp]
-            kc[b, 0:16] = lax.dot_general(
-                pot[b], xd[b].reshape(512, 512), NT, preferred_element_type=F32
-            ).reshape(16, 16, 512)
-        for v in range(4):
-            for u in range(4):
-                for c in range(2):
+        k1[half, 0:16] = lax.dot_general(
+            pot[1], xd[rp].reshape(512, 512), NT, preferred_element_type=F32
+        ).reshape(16, 16, 512)
+        for ref, c in ((kp, 1 - core), (s1, core)):
+            for v in range(4):
+                for u in range(4):
                     nb = 2 * (NX * v + u if half == 0 else NX * u + v) + c
-                    kp[c, rp, v, u] = kc[0, inv[0, nb]] + kc[1, inv[1, nb]]
-        d_copy(rp).start()
+                    ref[rp, v, u] = k0[rp, inv[0, nb]] + k1[half, inv[1, nb]]
+            if ref is kp:
+                d_copy(rp).start()
 
     def send_slice(half, rp):
         d_copy(rp).wait_recv()
-        s1[rp] = kp[core, rp] + d0[rp]
+        s1[rp] = s1[rp] + d0[rp]
         for m in (0, 3, 1, 4):
             a_copy(half, rp, m).start()
 
@@ -287,90 +301,61 @@
 
     finish.append(finish_a)
 
+    def combine_slice(half, rp):
+        u = first[half]
+        a_copy(half, rp, 0).wait_recv()
+        cb[0, rp] = rb[0, rp] + s1[rp, :, mod(u + 1, 4), 0:8]
+        a_copy(half, rp, 2).start()
+        a_copy(half, rp, 3).wait_recv()
+        cb[1, rp] = rb[3, rp] + s1[rp, :, mod(u + 3, 4), 8:16]
+        a_copy(half, rp, 5).start()
+
+    def second_slice(half, rp):
+        u = first[half]
+        for m in (1, 4, 2, 5):
+            a_copy(half, rp, m).wait_recv()
+        t1[rp, :, 0:8] = s1[rp, :, u, 0:8] + rb[4, rp] + rb[2, rp]
+        t1[rp, :, 8:16] = s1[rp, :, u, 8:16] + rb[1, rp] + rb[5, rp]
+        for m in range(3):
+            b_copy(half, rp, m).start()
+
+    def z_copy(rp):
+        return remote(z1.at[rp], out.at[r], z_s.at[rp], z_r.at[r], at_z(rp))
+
+    def last_slice(half, rp):
+        for m in (1, 2, 0):
+            b_copy(half, rp, m).wait_recv()
+        total = t1[rp, second[half]] + rb2[1, rp] + rb2[2, rp] + rb2[0, rp]
+        z1[rp] = total
+
+        @pl.when(rp != r)
+        def _():
+            z_copy(rp).start()
+
+    plan = (
+        (make_slice, 0), (make_slice, 1), (send_slice, 0), (make_slice, 2), (send_slice, 1), (make_slice, 3),
+        (send_slice, 2), (combine_slice, 0), (send_slice, 3), (combine_slice, 1), (combine_slice, 2),
+        (second_slice, 0), (combine_slice, 3), (second_slice, 1), (second_slice, 2), (last_slice, 0),
+        (second_slice, 3), (last_slice, 1), (last_slice, 2), (last_slice, 3),
+    )
+    for stage, p in plan:
+        stage(0, p)
+        stage(1, p + 4)
+
+    out[r] = z1[r]
+
+    @pl.loop(1, NZ)
+    def _(k):
+        source = mod(r + k, NZ)
+        remote(z1.at[source], out.at[source], z_s.at[source], z_r.at[source], at_z(source)).wait_recv()
+
+    for waits in finish:
+        waits()
+
     @pl.loop(0, 4)
     def _(p):
         for half in range(2):
-            make_slice(half, p + 4 * half)
-
-            @pl.when(p > 0)
-            def _():
-                send_slice(half, p + 4 * half - 1)
-
-    for half in range(2):
-        send_slice(half, 3 + 4 * half)
-
-
-    @pl.loop(0, 4)
-    def _(p):
-        for half in range(2):
-            rp = p + 4 * half
-            u = first[half]
-            a_copy(half, rp, 0).wait_recv()
-            cb[0, rp] = rb[0, rp] + s1[rp, :, mod(u + 1, 4), 0:8]
-            a_copy(half, rp, 2).start()
-            a_copy(half, rp, 3).wait_recv()
-            cb[1, rp] = rb[3, rp] + s1[rp, :, mod(u + 3, 4), 8:16]
-            a_copy(half, rp, 5).start()
-
-    @pl.loop(0, 4)
-    def _(p):
-        for half in range(2):
-            rp = p + 4 * half
-            u = first[half]
-            for m in (1, 4, 2, 5):
-                a_copy(half, rp, m).wait_recv()
-            t1[rp, :, 0:8] = s1[rp, :, u, 0:8] + rb[4, rp] + rb[2, rp]
-            t1[rp, :, 8:16] = s1[rp, :, u, 8:16] + rb[1, rp] + rb[5, rp]
-            for m in (0, 3, 1, 4):
-                b_copy(half, rp, m).start()
-
-    @pl.loop(0, 4)
-    def _(p):
-        for half in range(2):
-            rp = p + 4 * half
-            u = second[half]
-            b_copy(half, rp, 0).wait_recv()
-            cb2[0, rp] = rb2[0, rp] + t1[rp, mod(u + 1, 4), 0:8]
-            b_copy(half, rp, 2).start()
-            b_copy(half, rp, 3).wait_recv()
-            cb2[1, rp] = rb2[3, rp] + t1[rp, mod(u + 3, 4), 8:16]
-            b_copy(half, rp, 5).start()
-
-    def z_copy(rp):
-        return remote(z1.at[rp], zr.at[r], z_s.at[rp], z_r.at[r], at_z(rp))
-
-    @pl.loop(0, 4)
-    def _(p):
-        for half in range(2):
-            rp = p + 4 * half
-            u = second[half]
-            for m in (1, 4, 2, 5):
-                b_copy(half, rp, m).wait_recv()
-            z1[rp, 0:8] = t1[rp, u, 0:8] + rb2[4, rp] + rb2[2, rp]
-            z1[rp, 8:16] = t1[rp, u, 8:16] + rb2[1, rp] + rb2[5, rp]
-
-            @pl.when(rp != r)
-            def _():
-                z_copy(rp).start()
-
-    zr[r] = z1[r]
-
-    @pl.loop(1, NZ)
-    def _(k):
-        source = mod(r + k, NZ)
-        remote(z1.at[source], zr.at[source], z_s.at[source], z_r.at[source], at_z(source)).wait_recv()
-
-    for c in range(4):
-        block = zr[:, :, 128 * c : 128 * (c + 1)].reshape(128, 128)
-        out[8 * c : 8 * c + 8] = block.T.reshape(8, 16, 128)
-
-    for waits in finish:
-        waits()
-
-    @pl.loop(0, 4)
-    def _(p):
-        for half in range(2):
-            for m in range(6):
+            for m in range(3):
                 b_copy(half, p + 4 * half, m).wait_send()
 
     @pl.loop(1, NZ)
@@ -380,12 +365,13 @@
 
 def body(density, basis_values, grid_points, grid_weights, screened_blocks):
     vmem = pl.BlockSpec(memory_space=pltpu.VMEM)
+    hbm = pl.BlockSpec(memory_space=pl.ANY)
     smem = pl.BlockSpec(memory_space=pltpu.SMEM)
     dma = pltpu.SemaphoreType.DMA
-    return pl.pallas_call(
+    rows = pl.pallas_call(
         kernel,
-        out_shape=jax.ShapeDtypeStruct((32, 16, 128), F32),
-        in_specs=[smem, vmem, vmem, vmem, vmem],
+        out_shape=jax.ShapeDtypeStruct((8, 16, 512), F32),
+        in_specs=[smem, hbm, hbm, vmem, vmem],
         out_specs=vmem,
         scratch_shapes=[
             pltpu.SMEM((2, 32), jnp.int32),
@@ -400,18 +386,18 @@
             pltpu.VMEM((2, 8, 64, 256), BF16),
             pltpu.VMEM((2, 8, 64, 256), BF16),
             pltpu.VMEM((2, 256, 512), BF16),
-            pltpu.VMEM((2, 32, 16, 512), BF16),
+            pltpu.VMEM((9, 32, 16, 512), BF16),
+            pltpu.VMEM((8, 17, 16, 512), F32),
             pltpu.VMEM((2, 17, 16, 512), F32),
-            pltpu.VMEM((2, 8, 4, 4, 16, 512), F32),
+            pltpu.VMEM((8, 4, 4, 16, 512), F32),
             pltpu.VMEM((8, 4, 4, 16, 512), F32),
             pltpu.VMEM((8, 4, 4, 16, 512), F32),
             pltpu.VMEM((6, 8, 4, 8, 512), F32),
             pltpu.VMEM((2, 8, 4, 8, 512), F32),
             pltpu.VMEM((8, 4, 16, 512), F32),
-            pltpu.VMEM((6, 8, 8, 512), F32),
-            pltpu.VMEM((2, 8, 8, 512), F32),
+            pltpu.VMEM((3, 8, 16, 512), F32),
             pltpu.VMEM((8, 16, 512), F32),
-            pltpu.VMEM((8, 16, 512), F32),
+            dma((3,)),
             dma((2, 4, 2)), dma((2, 4, 2)),
             dma((2, 2, 2)), dma((2, 2, 2)),
             dma((4,)), dma((4,)),
@@ -419,7 +405,7 @@
             dma((2, 8)), dma((2, 8)),
             dma((8,)), dma((8,)),
             dma((6, 8)), dma((6, 8)),
-            dma((6, 8)), dma((6, 8)),
+            dma((3, 8)), dma((3, 8)),
             dma((8,)), dma((8,)),
         ],
         compiler_params=pltpu.CompilerParams(
@@ -428,6 +414,7 @@
         cost_estimate=pl.CostEstimate(flops=4_000_000_000, bytes_accessed=2_000_000, transcendentals=100_000),
         name="exchange",
     )(screened_blocks, density, basis_values, jnp.transpose(grid_points, (1, 0, 2)), grid_weights)
+    return rows.reshape(128, 512).T.reshape(32, 16, 128)
 
 
 def solution(mesh):

time: 113 us -> 112 us (level)
  Pallas kernels: 111 us -> 109 us
    transpose x0 -> x1, local copies, waits for them, and re-layouts: none -> 1.79 us  [body(): return rows.reshape(128, 512).T.reshape(32, 16, 128)]
    unnamed x1 -> x0, local copies, waits for them, and re-layouts: 1.67 us -> none
    pallas_call x1, Pallas kernels: 111 us -> 109 us  [body(): pl.pallas_call(kernel, out_shape=jax.ShapeDtypeStruct((8, 16, 512), F32),...]
where the time goes in v3:
time: 112 us; the launch traced here: 111 us
  Pallas kernels  109 us (97%)
  local copies, waits for them, and re-layouts  1.79 us (2%)
    pallas_call x1, Pallas kernels, body(): pl.pallas_call(kernel, out_shape=jax.ShapeDtypeStruct((8, 16, 512), F32),...  109 us

profile of v3, /device:TPU:96, one launch (start us, length us, event | category | flops | bytes accessed | tf_op | source)
XLA Modules:
  0.0 111.0 jit_solution(2704717685543058606)
XLA Ops:
  0.0 109.2 %exchange.1 = f32[8,16,512]{2,1,0:T(8,128)} custom-call(s32[2,16]{1,0:T(2,128)} %sel.1, bf16[32,16,128]{2,1,0:T(8,128)(2,1)} %dens.1, bf16[2,16,16,512]{3,2,1,0:T(8,128)(2,1)} %xin.1, f32[3,2,512]{2,1,0:T(2,128)} %bitcast.6, f32[2,512]{1,0:T(2,128)} %wts.1), custom_call_target="tpu_custom_call" | custom-call | flops 4000000000 | bytes 2000000 | tf_op jit(solution)/shard_map/exchange/pallas_call | solution.py:371
  109.2 1.8 %copy.6 = f32[512,128]{1,0:T(8,128)} copy(f32[512,128]{0,1:T(8,128)} %bitcast.5) | data formatting | bytes 524288 | tf_op jit(solution)/shard_map/transpose | solution.py:417

commit v4 on v3

--- a/solution.py
+++ b/solution.py
@@ -13,15 +13,27 @@
 F32 = jnp.float32
 NT = (((1,), (1,)), ((), ()))
 FAR_FIRST = (4, 3, 5, 2, 6, 1, 7)
+LIMIT = 32767.0
+TINY = 1e-33
 
 
 def mod(a, n):
     return lax.rem(a, n)
 
 
+def encode(values, codes, scales):
+    largest = jnp.max(jnp.abs(values), axis=0, keepdims=True)
+    codes[...] = jnp.round(values * (LIMIT / jnp.maximum(largest, TINY))).astype(jnp.int32).astype(jnp.int16)
+    scales[...] = largest * (1.0 / LIMIT)
+
+
+def decode(codes, scales):
+    return codes[...].astype(jnp.int32).astype(F32) * scales[...]
+
+
 def kernel(
     sel, dens, xin, pts, wts, out,
-    inv, pg, xg, psel, tcol, scale, wcol, fs, fr, ps, pr, pot, xd, k0, k1, kp, d0, s1, rb, cb, t1, rb2, z1,
+    inv, pg, xg, psel, tcol, scale, wcol, fs, fr, ps, pr, pot, xd, k0, k1, kp, kq, ks, s1, aq, az, t1, bq, bz, z1,
     o_s, x_s, x_r, p_s, p_r, q_s, q_r, f_s, f_r, m_s, m_r, d_s, d_r, a_s, a_r, b_s, b_r, z_s, z_r,
 ):
     g = lax.axis_index("grid")
@@ -249,10 +261,27 @@
 
     first = (x, y)
     second = (y, x)
-    low, high = pl.ds(0, 8), pl.ds(8, 8)
+
+    def pair(codes, scales, code_sems, scale_sems, device):
+        return (remote(*codes, *code_sems, device), remote(*scales, *scale_sems, device))
 
     def d_copy(rp):
-        return remote(kp.at[rp], d0.at[rp], d_s.at[rp], d_r.at[rp], partner)
+        return pair(
+            (kq.at[0, rp], kq.at[1, rp]), (ks.at[0, rp], ks.at[1, rp]),
+            (d_s.at[0, rp], d_r.at[0, rp]), (d_s.at[1, rp], d_r.at[1, rp]), partner,
+        )
+
+    def start(copies):
+        for copy in copies:
+            copy.start()
+
+    def wait_recv(copies):
+        for copy in copies:
+            copy.wait_recv()
+
+    def wait_send(copies):
+        for copy in copies:
+            copy.wait_send()
 
     def along(half, stage, shift):
         if half == stage:
@@ -260,18 +289,25 @@
         return at_plane(x, mod(y + shift, NY))
 
     def a_copy(half, rp, m):
-        u = first[half]
-        nxt, opp, prv = mod(u + 1, 4), mod(u + 2, 4), mod(u + 3, 4)
-        src = (
-            s1.at[rp, :, opp, low], s1.at[rp, :, nxt, high], cb.at[0, rp],
-            s1.at[rp, :, opp, high], s1.at[rp, :, prv, low], cb.at[1, rp],
-        )[m]
-        return remote(src, rb.at[m, rp], a_s.at[m, rp], a_r.at[m, rp], along(half, 0, 1 if m < 3 else 3))
+        return pair(
+            (aq.at[0, m, rp], aq.at[1, m, rp]), (az.at[0, m, rp], az.at[1, m, rp]),
+            (a_s.at[0, m, rp], a_r.at[0, m, rp]), (a_s.at[1, m, rp], a_r.at[1, m, rp]),
+            along(half, 0, 1 if m < 3 else 3),
+        )
+
+    def a_send(half, rp, m, values):
+        encode(values.reshape(32, 512), aq.at[0, m, rp], az.at[0, m, rp])
+        start(a_copy(half, rp, m))
+
+    def a_value(rp, m):
+        return decode(aq.at[1, m, rp], az.at[1, m, rp]).reshape(4, 8, 512)
 
     def b_copy(half, rp, m):
-        shift = (2, 1, 3)[m]
-        src = t1.at[rp, mod(second[half] + shift, 4)]
-        return remote(src, rb2.at[m, rp], b_s.at[m, rp], b_r.at[m, rp], along(half, 1, shift))
+        return pair(
+            (bq.at[0, m, rp], bq.at[1, m, rp]), (bz.at[0, m, rp], bz.at[1, m, rp]),
+            (b_s.at[0, m, rp], b_r.at[0, m, rp]), (b_s.at[1, m, rp], b_r.at[1, m, rp]),
+            along(half, 1, (2, 1, 3)[m]),
+        )
 
     def make_slice(half, rp):
         k1[half, 0:16] = lax.dot_general(
@@ -283,49 +319,60 @@
                     nb = 2 * (NX * v + u if half == 0 else NX * u + v) + c
                     ref[rp, v, u] = k0[rp, inv[0, nb]] + k1[half, inv[1, nb]]
             if ref is kp:
-                d_copy(rp).start()
+                for part in range(8):
+                    encode(
+                        kp[rp, part // 2, 2 * (part % 2) : 2 * (part % 2) + 2].reshape(32, 512),
+                        kq.at[0, rp, pl.ds(32 * part, 32)], ks.at[0, rp, part],
+                    )
+                start(d_copy(rp))
 
     def send_slice(half, rp):
-        d_copy(rp).wait_recv()
-        s1[rp] = s1[rp] + d0[rp]
-        for m in (0, 3, 1, 4):
-            a_copy(half, rp, m).start()
+        wait_recv(d_copy(rp))
+        for part in range(8):
+            s1[rp, part // 2, 2 * (part % 2) : 2 * (part % 2) + 2] += decode(
+                kq.at[1, rp, pl.ds(32 * part, 32)], ks.at[1, rp, part]
+            ).reshape(2, 16, 512)
+        u = first[half]
+        a_send(half, rp, 0, s1[rp, :, mod(u + 2, 4), 0:8])
+        a_send(half, rp, 3, s1[rp, :, mod(u + 2, 4), 8:16])
+        a_send(half, rp, 1, s1[rp, :, mod(u + 1, 4), 8:16])
+        a_send(half, rp, 4, s1[rp, :, mod(u + 3, 4), 0:8])
 
     def finish_a():
         @pl.loop(0, 4)
         def _(p):
             for half in range(2):
-                d_copy(p + 4 * half).wait_send()
+                wait_send(d_copy(p + 4 * half))
                 for m in range(6):
-                    a_copy(half, p + 4 * half, m).wait_send()
+                    wait_send(a_copy(half, p + 4 * half, m))
 
     finish.append(finish_a)
 
     def combine_slice(half, rp):
         u = first[half]
-        a_copy(half, rp, 0).wait_recv()
-        cb[0, rp] = rb[0, rp] + s1[rp, :, mod(u + 1, 4), 0:8]
-        a_copy(half, rp, 2).start()
-        a_copy(half, rp, 3).wait_recv()
-        cb[1, rp] = rb[3, rp] + s1[rp, :, mod(u + 3, 4), 8:16]
-        a_copy(half, rp, 5).start()
+        wait_recv(a_copy(half, rp, 0))
+        a_send(half, rp, 2, a_value(rp, 0) + s1[rp, :, mod(u + 1, 4), 0:8])
+        wait_recv(a_copy(half, rp, 3))
+        a_send(half, rp, 5, a_value(rp, 3) + s1[rp, :, mod(u + 3, 4), 8:16])
 
     def second_slice(half, rp):
         u = first[half]
         for m in (1, 4, 2, 5):
-            a_copy(half, rp, m).wait_recv()
-        t1[rp, :, 0:8] = s1[rp, :, u, 0:8] + rb[4, rp] + rb[2, rp]
-        t1[rp, :, 8:16] = s1[rp, :, u, 8:16] + rb[1, rp] + rb[5, rp]
+            wait_recv(a_copy(half, rp, m))
+        t1[rp, :, 0:8] = s1[rp, :, u, 0:8] + a_value(rp, 4) + a_value(rp, 2)
+        t1[rp, :, 8:16] = s1[rp, :, u, 8:16] + a_value(rp, 1) + a_value(rp, 5)
         for m in range(3):
-            b_copy(half, rp, m).start()
+            encode(t1[rp, mod(second[half] + (2, 1, 3)[m], 4)], bq.at[0, m, rp], bz.at[0, m, rp])
+            start(b_copy(half, rp, m))
 
     def z_copy(rp):
         return remote(z1.at[rp], out.at[r], z_s.at[rp], z_r.at[r], at_z(rp))
 
     def last_slice(half, rp):
+        total = t1[rp, second[half]]
         for m in (1, 2, 0):
-            b_copy(half, rp, m).wait_recv()
-        total = t1[rp, second[half]] + rb2[1, rp] + rb2[2, rp] + rb2[0, rp]
+            wait_recv(b_copy(half, rp, m))
+            total = total + decode(bq.at[1, m, rp], bz.at[1, m, rp])
         z1[rp] = total
 
         @pl.when(rp != r)
@@ -356,7 +403,7 @@
     def _(p):
         for half in range(2):
             for m in range(3):
-                b_copy(half, p + 4 * half, m).wait_send()
+                wait_send(b_copy(half, p + 4 * half, m))
 
     @pl.loop(1, NZ)
     def _(k):
@@ -390,12 +437,14 @@
             pltpu.VMEM((8, 17, 16, 512), F32),
             pltpu.VMEM((2, 17, 16, 512), F32),
             pltpu.VMEM((8, 4, 4, 16, 512), F32),
+            pltpu.VMEM((2, 8, 256, 512), jnp.int16),
+            pltpu.VMEM((2, 8, 8, 1, 512), F32),
             pltpu.VMEM((8, 4, 4, 16, 512), F32),
-            pltpu.VMEM((8, 4, 4, 16, 512), F32),
-            pltpu.VMEM((6, 8, 4, 8, 512), F32),
-            pltpu.VMEM((2, 8, 4, 8, 512), F32),
+            pltpu.VMEM((2, 6, 8, 32, 512), jnp.int16),
+            pltpu.VMEM((2, 6, 8, 1, 512), F32),
             pltpu.VMEM((8, 4, 16, 512), F32),
-            pltpu.VMEM((3, 8, 16, 512), F32),
+            pltpu.VMEM((2, 3, 8, 16, 512), jnp.int16),
+            pltpu.VMEM((2, 3, 8, 1, 512), F32),
             pltpu.VMEM((8, 16, 512), F32),
             dma((3,)),
             dma((2, 4, 2)), dma((2, 4, 2)),
@@ -403,9 +452,9 @@
             dma((4,)), dma((4,)),
             dma((2, 8)), dma((2, 8)),
             dma((2, 8)), dma((2, 8)),
-            dma((8,)), dma((8,)),
-            dma((6, 8)), dma((6, 8)),
-            dma((3, 8)), dma((3, 8)),
+            dma((2, 8)), dma((2, 8)),
+            dma((2, 6, 8)), dma((2, 6, 8)),
+            dma((2, 3, 8)), dma((2, 3, 8)),
             dma((8,)), dma((8,)),
         ],
         compiler_params=pltpu.CompilerParams(

time: 112 us -> 103 us (0.920)
  Pallas kernels: 109 us -> 101 us
    pallas_call x1, Pallas kernels: 109 us -> 101 us  [body(): pl.pallas_call(kernel, out_shape=jax.ShapeDtypeStruct((8, 16, 512), F32),...]
where the time goes in v4:
time: 103 us; the launch traced here: 102 us
  Pallas kernels  101 us (98%)
  local copies, waits for them, and re-layouts  1.79 us (2%)
    pallas_call x1, Pallas kernels, body(): pl.pallas_call(kernel, out_shape=jax.ShapeDtypeStruct((8, 16, 512), F32),...  101 us

profile of v4, /device:TPU:96, one launch (start us, length us, event | category | flops | bytes accessed | tf_op | source)
XLA Modules:
  0.0 102.4 jit_solution(4530609561953206771)
XLA Ops:
  0.0 100.6 %exchange.1 = f32[8,16,512]{2,1,0:T(8,128)} custom-call(s32[2,16]{1,0:T(2,128)} %sel.1, bf16[32,16,128]{2,1,0:T(8,128)(2,1)} %dens.1, bf16[2,16,16,512]{3,2,1,0:T(8,128)(2,1)} %xin.1, f32[3,2,512]{2,1,0:T(2,128)} %bitcast.6, f32[2,512]{1,0:T(2,128)} %wts.1), custom_call_target="tpu_custom_call" | custom-call | flops 4000000000 | bytes 2000000 | tf_op jit(solution)/shard_map/exchange/pallas_call | solution.py:418
  100.6 1.8 %copy.6 = f32[512,128]{1,0:T(8,128)} copy(f32[512,128]{0,1:T(8,128)} %bitcast.5) | data formatting | bytes 524288 | tf_op jit(solution)/shard_map/transpose | solution.py:466

commit v5 on v4

--- a/solution.py
+++ b/solution.py
@@ -14,7 +14,7 @@
 NT = (((1,), (1,)), ((), ()))
 FAR_FIRST = (4, 3, 5, 2, 6, 1, 7)
 LIMIT = 32767.0
-TINY = 1e-33
+TINY = 1.2e-38
 
 
 def mod(a, n):
@@ -23,12 +23,13 @@
 
 def encode(values, codes, scales):
     largest = jnp.max(jnp.abs(values), axis=0, keepdims=True)
-    codes[...] = jnp.round(values * (LIMIT / jnp.maximum(largest, TINY))).astype(jnp.int32).astype(jnp.int16)
-    scales[...] = largest * (1.0 / LIMIT)
+    parts = values * (1.0 / jnp.maximum(largest, TINY))
+    codes[...] = jnp.round(parts * LIMIT).astype(jnp.int32).astype(jnp.int16)
+    scales[...] = largest
 
 
 def decode(codes, scales):
-    return codes[...].astype(jnp.int32).astype(F32) * scales[...]
+    return (codes[...].astype(jnp.int32).astype(F32) * (1.0 / LIMIT)) * scales[...]
 
 
 def kernel(
@@ -74,7 +75,7 @@
         shard = mod(r + (NZ - t if d == 0 else t), NZ)
         part = pl.ds(0, 16) if t < 3 else pl.ds(8 * d, 8)
         dst = xg.at[b, part, shard]
-        return remote(dst, dst, x_s.at[d, t, b], x_r.at[d, t, b], up if d == 0 else down)
+        return remote(dst, dst, x_s.at[0], x_r.at[d, t, b], up if d == 0 else down)
 
     def x_send(t, b):
         for d in range(2):
@@ -170,10 +171,9 @@
         pq_copy(k).wait_recv()
 
     def finish_gathers():
+        sent = xg.at[:, pl.ds(0, 16), pl.ds(0, 7)]
+        remote(sent, sent, x_s.at[0], x_r.at[0, 0, 0], up).wait_send()
         for d in range(2):
-            for t in range(4):
-                for b in range(2):
-                    x_copy(d, t, b).wait_send()
             for t in range(2):
                 px_copy(d, t).wait_send()
                 py_copy(d, t).wait_send()
@@ -194,7 +194,7 @@
 
     def f_copy(b, k):
         to = mod(r + k, NZ)
-        return remote(fs.at[b, to], fr.at[b, r], f_s.at[b, k], f_r.at[b, k], at_z(to))
+        return remote(fs.at[b, to], fr.at[b, r], f_s.at[0], f_r.at[b], at_z(to))
 
     for b in range(2):
         for d in range(2):
@@ -208,19 +208,17 @@
         fr[b, r] = fs[b, r]
 
     def finish_f():
-        for b in range(2):
-            for k in FAR_FIRST:
-                f_copy(b, k).wait_send()
+        some = pl.ds(0, 7)
+        remote(fs.at[:, some], fr.at[:, some], f_s.at[0], f_r.at[0], up).wait_send()
 
     finish.append(finish_f)
 
     def m_copy(b, k):
         to = mod(r + k, NZ)
-        return remote(ps.at[b, to], pr.at[b, r], m_s.at[b, k], m_r.at[b, k], at_z(to))
+        return remote(ps.at[b, to], pr.at[b, r], m_s.at[0], m_r.at[b], at_z(to))
 
     for b in range(2):
-        for k in FAR_FIRST:
-            f_copy(b, k).wait_recv()
+        remote(fs.at[b, pl.ds(0, 7)], fr.at[b, pl.ds(0, 7)], f_s.at[0], f_r.at[b], up).wait_recv()
         inter = jnp.zeros((64, 512), F32)
         for s in range(8):
             inter = inter + jnp.dot(fr[b, s], xg[b, 0:16, s].reshape(256, 512), preferred_element_type=F32)
@@ -234,15 +232,13 @@
         pr[b, r] = ps[b, r]
 
     def finish_m():
-        for b in range(2):
-            for k in FAR_FIRST:
-                m_copy(b, k).wait_send()
+        some = pl.ds(0, 7)
+        remote(ps.at[:, some], pr.at[:, some], m_s.at[0], m_r.at[0], up).wait_send()
 
     finish.append(finish_m)
 
     def potential(b):
-        for k in FAR_FIRST:
-            m_copy(b, k).wait_recv()
+        remote(ps.at[b, pl.ds(0, 7)], pr.at[b, pl.ds(0, 7)], m_s.at[0], m_r.at[b], up).wait_recv()
         pot[b] = pr[b].reshape(512, 256).T
 
     potential(0)
@@ -268,7 +264,7 @@
     def d_copy(rp):
         return pair(
             (kq.at[0, rp], kq.at[1, rp]), (ks.at[0, rp], ks.at[1, rp]),
-            (d_s.at[0, rp], d_r.at[0, rp]), (d_s.at[1, rp], d_r.at[1, rp]), partner,
+            (d_s.at[0], d_r.at[0, rp]), (d_s.at[1], d_r.at[1, rp]), partner,
         )
 
     def start(copies):
@@ -288,25 +284,23 @@
             return at_plane(mod(x + shift, NX), y)
         return at_plane(x, mod(y + shift, NY))
 
-    def a_copy(half, rp, m):
+    def a_pair(rp, which, group, device):
         return pair(
-            (aq.at[0, m, rp], aq.at[1, m, rp]), (az.at[0, m, rp], az.at[1, m, rp]),
-            (a_s.at[0, m, rp], a_r.at[0, m, rp]), (a_s.at[1, m, rp], a_r.at[1, m, rp]),
-            along(half, 0, 1 if m < 3 else 3),
+            (aq.at[0, which, rp], aq.at[1, which, rp]), (az.at[0, which, rp], az.at[1, which, rp]),
+            (a_s.at[0], a_r.at[0, group, rp]), (a_s.at[1], a_r.at[1, group, rp]), device,
         )
 
     def a_send(half, rp, m, values):
         encode(values.reshape(32, 512), aq.at[0, m, rp], az.at[0, m, rp])
-        start(a_copy(half, rp, m))
+        start(a_pair(rp, m, min(m, 2), along(half, 0, 1 if m % 2 == 0 else 3)))
 
     def a_value(rp, m):
         return decode(aq.at[1, m, rp], az.at[1, m, rp]).reshape(4, 8, 512)
 
-    def b_copy(half, rp, m):
+    def b_pair(rp, which, device):
         return pair(
-            (bq.at[0, m, rp], bq.at[1, m, rp]), (bz.at[0, m, rp], bz.at[1, m, rp]),
-            (b_s.at[0, m, rp], b_r.at[0, m, rp]), (b_s.at[1, m, rp], b_r.at[1, m, rp]),
-            along(half, 1, (2, 1, 3)[m]),
+            (bq.at[0, which, rp], bq.at[1, which, rp]), (bz.at[0, which, rp], bz.at[1, which, rp]),
+            (b_s.at[0], b_r.at[0, rp]), (b_s.at[1], b_r.at[1, rp]), device,
         )
 
     def make_slice(half, rp):
@@ -334,44 +328,49 @@
             ).reshape(2, 16, 512)
         u = first[half]
         a_send(half, rp, 0, s1[rp, :, mod(u + 2, 4), 0:8])
-        a_send(half, rp, 3, s1[rp, :, mod(u + 2, 4), 8:16])
-        a_send(half, rp, 1, s1[rp, :, mod(u + 1, 4), 8:16])
-        a_send(half, rp, 4, s1[rp, :, mod(u + 3, 4), 0:8])
+        a_send(half, rp, 1, s1[rp, :, mod(u + 2, 4), 8:16])
+        a_send(half, rp, 2, s1[rp, :, mod(u + 1, 4), 8:16])
+        a_send(half, rp, 3, s1[rp, :, mod(u + 3, 4), 0:8])
 
     def finish_a():
-        @pl.loop(0, 4)
-        def _(p):
-            for half in range(2):
-                wait_send(d_copy(p + 4 * half))
-                for m in range(6):
-                    wait_send(a_copy(half, p + 4 * half, m))
+        def whole(codes, scales, send, recv):
+            first_of = (0,) * (len(recv.shape) - 1)
+            wait_send(
+                pair(
+                    (codes.at[0], codes.at[1]), (scales.at[0], scales.at[1]),
+                    (send.at[0], recv.at[(0, *first_of)]), (send.at[1], recv.at[(1, *first_of)]), partner,
+                )
+            )
+
+        whole(kq, ks, d_s, d_r)
+        whole(aq, az, a_s, a_r)
+        whole(bq, bz, b_s, b_r)
 
     finish.append(finish_a)
 
     def combine_slice(half, rp):
         u = first[half]
-        wait_recv(a_copy(half, rp, 0))
-        a_send(half, rp, 2, a_value(rp, 0) + s1[rp, :, mod(u + 1, 4), 0:8])
-        wait_recv(a_copy(half, rp, 3))
-        a_send(half, rp, 5, a_value(rp, 3) + s1[rp, :, mod(u + 3, 4), 8:16])
+        wait_recv(a_pair(rp, 0, 0, partner))
+        a_send(half, rp, 4, a_value(rp, 0) + s1[rp, :, mod(u + 1, 4), 0:8])
+        wait_recv(a_pair(rp, 1, 1, partner))
+        a_send(half, rp, 5, a_value(rp, 1) + s1[rp, :, mod(u + 3, 4), 8:16])
 
     def second_slice(half, rp):
         u = first[half]
-        for m in (1, 4, 2, 5):
-            wait_recv(a_copy(half, rp, m))
-        t1[rp, :, 0:8] = s1[rp, :, u, 0:8] + a_value(rp, 4) + a_value(rp, 2)
-        t1[rp, :, 8:16] = s1[rp, :, u, 8:16] + a_value(rp, 1) + a_value(rp, 5)
+        wait_recv(a_pair(rp, pl.ds(2, 4), 2, partner))
+        t1[rp, :, 0:8] = s1[rp, :, u, 0:8] + a_value(rp, 3) + a_value(rp, 4)
+        t1[rp, :, 8:16] = s1[rp, :, u, 8:16] + a_value(rp, 2) + a_value(rp, 5)
         for m in range(3):
             encode(t1[rp, mod(second[half] + (2, 1, 3)[m], 4)], bq.at[0, m, rp], bz.at[0, m, rp])
-            start(b_copy(half, rp, m))
+            start(b_pair(rp, m, along(half, 1, (2, 1, 3)[m])))
 
     def z_copy(rp):
-        return remote(z1.at[rp], out.at[r], z_s.at[rp], z_r.at[r], at_z(rp))
+        return remote(z1.at[rp], out.at[r], z_s.at[0], z_r.at[0], at_z(rp))
 
     def last_slice(half, rp):
         total = t1[rp, second[half]]
-        for m in (1, 2, 0):
-            wait_recv(b_copy(half, rp, m))
+        wait_recv(b_pair(rp, pl.ds(0, 3), partner))
+        for m in range(3):
             total = total + decode(bq.at[1, m, rp], bz.at[1, m, rp])
         z1[rp] = total
 
@@ -391,23 +390,13 @@
 
     out[r] = z1[r]
 
-    @pl.loop(1, NZ)
-    def _(k):
-        source = mod(r + k, NZ)
-        remote(z1.at[source], out.at[source], z_s.at[source], z_r.at[source], at_z(source)).wait_recv()
+    others = remote(z1.at[pl.ds(0, 7)], out.at[pl.ds(0, 7)], z_s.at[0], z_r.at[0], up)
+    others.wait_recv()
 
     for waits in finish:
         waits()
 
-    @pl.loop(0, 4)
-    def _(p):
-        for half in range(2):
-            for m in range(3):
-                wait_send(b_copy(half, p + 4 * half, m))
-
-    @pl.loop(1, NZ)
-    def _(k):
-        z_copy(mod(r + k, NZ)).wait_send()
+    others.wait_send()
 
 
 def body(density, basis_values, grid_points, grid_weights, screened_blocks):
@@ -447,15 +436,15 @@
             pltpu.VMEM((2, 3, 8, 1, 512), F32),
             pltpu.VMEM((8, 16, 512), F32),
             dma((3,)),
-            dma((2, 4, 2)), dma((2, 4, 2)),
+            dma((1,)), dma((2, 4, 2)),
             dma((2, 2, 2)), dma((2, 2, 2)),
             dma((4,)), dma((4,)),
-            dma((2, 8)), dma((2, 8)),
-            dma((2, 8)), dma((2, 8)),
-            dma((2, 8)), dma((2, 8)),
-            dma((2, 6, 8)), dma((2, 6, 8)),
-            dma((2, 3, 8)), dma((2, 3, 8)),
-            dma((8,)), dma((8,)),
+            dma((1,)), dma((2,)),
+            dma((1,)), dma((2,)),
+            dma((2,)), dma((2, 8)),
+            dma((2,)), dma((2, 3, 8)),
+            dma((2,)), dma((2, 8)),
+            dma((1,)), dma((1,)),
         ],
         compiler_params=pltpu.CompilerParams(
             collective_id=0, has_side_effects=True, vmem_limit_bytes=60 * 1024 * 1024

time: 103 us -> 99.3 us (0.964)
  Pallas kernels: 101 us -> 97.3 us
    pallas_call x1, Pallas kernels: 101 us -> 97.3 us  [body(): pl.pallas_call(kernel, out_shape=jax.ShapeDtypeStruct((8, 16, 512), F32),...]
where the time goes in v5:
time: 99.3 us; the launch traced here: 99.1 us
  Pallas kernels  97.3 us (98%)
  local copies, waits for them, and re-layouts  1.79 us (2%)
    pallas_call x1, Pallas kernels, body(): pl.pallas_call(kernel, out_shape=jax.ShapeDtypeStruct((8, 16, 512), F32),...  97.3 us

profile of v5, /device:TPU:96, one launch (start us, length us, event | category | flops | bytes accessed | tf_op | source)
XLA Modules:
  0.0 99.1 jit_solution(7598400317147722032)
XLA Ops:
  0.0 97.3 %exchange.1 = f32[8,16,512]{2,1,0:T(8,128)} custom-call(s32[2,16]{1,0:T(2,128)} %sel.1, bf16[32,16,128]{2,1,0:T(8,128)(2,1)} %dens.1, bf16[2,16,16,512]{3,2,1,0:T(8,128)(2,1)} %xin.1, f32[3,2,512]{2,1,0:T(2,128)} %bitcast.6, f32[2,512]{1,0:T(2,128)} %wts.1), custom_call_target="tpu_custom_call" | custom-call | flops 4000000000 | bytes 2000000 | tf_op jit(solution)/shard_map/exchange/pallas_call | solution.py:407
  97.3 1.8 %copy.6 = f32[512,128]{1,0:T(8,128)} copy(f32[512,128]{0,1:T(8,128)} %bitcast.5) | data formatting | bytes 524288 | tf_op jit(solution)/shard_map/transpose | solution.py:455

commit v6 on v5

--- a/solution.py
+++ b/solution.py
@@ -14,7 +14,7 @@
 NT = (((1,), (1,)), ((), ()))
 FAR_FIRST = (4, 3, 5, 2, 6, 1, 7)
 LIMIT = 32767.0
-TINY = 1.2e-38
+TINY = 4.8e-38
 
 
 def mod(a, n):
@@ -23,7 +23,7 @@
 
 def encode(values, codes, scales):
     largest = jnp.max(jnp.abs(values), axis=0, keepdims=True)
-    parts = values * (1.0 / jnp.maximum(largest, TINY))
+    parts = (values * 0.25) * (1.0 / (jnp.maximum(largest, TINY) * 0.25))
     codes[...] = jnp.round(parts * LIMIT).astype(jnp.int32).astype(jnp.int16)
     scales[...] = largest
 

time: 99.3 us -> 99.7 us (level)
  no operation moved by 1% of the time
where the time goes in v6:
time: 99.7 us; the launch traced here: 99.5 us
  Pallas kernels  97.7 us (98%)
  local copies, waits for them, and re-layouts  1.79 us (2%)
    pallas_call x1, Pallas kernels, body(): pl.pallas_call(kernel, out_shape=jax.ShapeDtypeStruct((8, 16, 512), F32),...  97.7 us

profile of v6, /device:TPU:96, one launch (start us, length us, event | category | flops | bytes accessed | tf_op | source)
XLA Modules:
  0.0 99.5 jit_solution(5375976267844700600)
XLA Ops:
  0.0 97.7 %exchange.1 = f32[8,16,512]{2,1,0:T(8,128)} custom-call(s32[2,16]{1,0:T(2,128)} %sel.1, bf16[32,16,128]{2,1,0:T(8,128)(2,1)} %dens.1, bf16[2,16,16,512]{3,2,1,0:T(8,128)(2,1)} %xin.1, f32[3,2,512]{2,1,0:T(2,128)} %bitcast.6, f32[2,512]{1,0:T(2,128)} %wts.1), custom_call_target="tpu_custom_call" | custom-call | flops 4000000000 | bytes 2000000 | tf_op jit(solution)/shard_map/exchange/pallas_call | solution.py:407
  97.7 1.8 %copy.6 = f32[512,128]{1,0:T(8,128)} copy(f32[512,128]{0,1:T(8,128)} %bitcast.5) | data formatting | bytes 524288 | tf_op jit(solution)/shard_map/transpose | solution.py:455

commit v7 on v6

--- a/solution.py
+++ b/solution.py
@@ -88,18 +88,18 @@
             ref = pg.at[y, x, core]
         else:
             ref = pg.at[y, mod(x + (3 if d == 0 else 1), NX), core, pl.ds(16 * d, 16)]
-        return remote(ref, ref, p_s.at[0, d, t], p_r.at[0, d, t], east if d == 0 else west)
+        return remote(ref, ref, p_s.at[0], p_r.at[0, d, t], east if d == 0 else west)
 
     def py_copy(d, t):
         if t == 0:
             ref = pg.at[y, :, core]
         else:
             ref = pg.at[mod(y + (3 if d == 0 else 1), NY), :, core, pl.ds(16 * d, 16)]
-        return remote(ref, ref, p_s.at[1, d, t], p_r.at[1, d, t], north if d == 0 else south)
+        return remote(ref, ref, p_s.at[1], p_r.at[1, d, t], north if d == 0 else south)
 
     def pq_copy(k):
         ref = pg.at[mod(y + k, NY), :, core]
-        return remote(ref, ref, q_s.at[k], q_r.at[k], partner)
+        return remote(ref, ref, q_s.at[0], q_r.at[0], partner)
 
     x_send(0, 0)
     own[2].wait()
@@ -167,18 +167,17 @@
 
     x_send(3, 1)
 
-    for k in range(4):
-        pq_copy(k).wait_recv()
+    half_grid = pg.at[:, :, core]
+    to_partner = remote(half_grid, pg.at[:, :, 1 - core], q_s.at[0], q_r.at[0], partner)
+    to_partner.wait_recv()
 
     def finish_gathers():
         sent = xg.at[:, pl.ds(0, 16), pl.ds(0, 7)]
         remote(sent, sent, x_s.at[0], x_r.at[0, 0, 0], up).wait_send()
-        for d in range(2):
-            for t in range(2):
-                px_copy(d, t).wait_send()
-                py_copy(d, t).wait_send()
-        for k in range(4):
-            pq_copy(k).wait_send()
+        line, plane = pg.at[0, pl.ds(0, 3), core], pg.at[pl.ds(0, 3), :, core]
+        remote(line, line, p_s.at[0], p_r.at[0, 0, 0], east).wait_send()
+        remote(plane, plane, p_s.at[1], p_r.at[1, 0, 0], north).wait_send()
+        to_partner.wait_send()
 
     finish.append(finish_gathers)
 
@@ -292,7 +291,7 @@
 
     def a_send(half, rp, m, values):
         encode(values.reshape(32, 512), aq.at[0, m, rp], az.at[0, m, rp])
-        start(a_pair(rp, m, min(m, 2), along(half, 0, 1 if m % 2 == 0 else 3)))
+        start(a_pair(rp, m, m // 2 if m < 2 else 1, along(half, 0, 1 if m % 2 == 0 else 3)))
 
     def a_value(rp, m):
         return decode(aq.at[1, m, rp], az.at[1, m, rp]).reshape(4, 8, 512)
@@ -350,14 +349,13 @@
 
     def combine_slice(half, rp):
         u = first[half]
-        wait_recv(a_pair(rp, 0, 0, partner))
+        wait_recv(a_pair(rp, pl.ds(0, 2), 0, partner))
         a_send(half, rp, 4, a_value(rp, 0) + s1[rp, :, mod(u + 1, 4), 0:8])
-        wait_recv(a_pair(rp, 1, 1, partner))
         a_send(half, rp, 5, a_value(rp, 1) + s1[rp, :, mod(u + 3, 4), 8:16])
 
     def second_slice(half, rp):
         u = first[half]
-        wait_recv(a_pair(rp, pl.ds(2, 4), 2, partner))
+        wait_recv(a_pair(rp, pl.ds(2, 4), 1, partner))
         t1[rp, :, 0:8] = s1[rp, :, u, 0:8] + a_value(rp, 3) + a_value(rp, 4)
         t1[rp, :, 8:16] = s1[rp, :, u, 8:16] + a_value(rp, 2) + a_value(rp, 5)
         for m in range(3):
@@ -437,12 +435,12 @@
             pltpu.VMEM((8, 16, 512), F32),
             dma((3,)),
             dma((1,)), dma((2, 4, 2)),
-            dma((2, 2, 2)), dma((2, 2, 2)),
-            dma((4,)), dma((4,)),
+            dma((2,)), dma((2, 2, 2)),
+            dma((1,)), dma((1,)),
             dma((1,)), dma((2,)),
             dma((1,)), dma((2,)),
             dma((2,)), dma((2, 8)),
-            dma((2,)), dma((2, 3, 8)),
+            dma((2,)), dma((2, 2, 8)),
             dma((2,)), dma((2, 8)),
             dma((1,)), dma((1,)),
         ],

time: 99.7 us -> 99.8 us (level)
  no operation moved by 1% of the time
where the time goes in v7:
time: 99.8 us; the launch traced here: 99.6 us
  Pallas kernels  97.8 us (98%)
  local copies, waits for them, and re-layouts  1.79 us (2%)
    pallas_call x1, Pallas kernels, body(): pl.pallas_call(kernel, out_shape=jax.ShapeDtypeStruct((8, 16, 512), F32),...  97.8 us

profile of v7, /device:TPU:96, one launch (start us, length us, event | category | flops | bytes accessed | tf_op | source)
XLA Modules:
  0.0 99.6 jit_solution(2943073208319832700)
XLA Ops:
  0.0 97.8 %exchange.1 = f32[8,16,512]{2,1,0:T(8,128)} custom-call(s32[2,16]{1,0:T(2,128)} %sel.1, bf16[32,16,128]{2,1,0:T(8,128)(2,1)} %dens.1, bf16[2,16,16,512]{3,2,1,0:T(8,128)(2,1)} %xin.1, f32[3,2,512]{2,1,0:T(2,128)} %bitcast.6, f32[2,512]{1,0:T(2,128)} %wts.1), custom_call_target="tpu_custom_call" | custom-call | flops 4000000000 | bytes 2000000 | tf_op jit(solution)/shard_map/exchange/pallas_call | solution.py:405
  97.8 1.8 %copy.6 = f32[512,128]{1,0:T(8,128)} copy(f32[512,128]{0,1:T(8,128)} %bitcast.5) | data formatting | bytes 524288 | tf_op jit(solution)/shard_map/transpose | solution.py:453
